TPU v7x, 32 devices: a whole 2x2x4 slice. The times are simulated.
32 devices in a mesh: grp: 2 (over y), theta: 8 (over z, x), phi: 2 (over core).
Axes of the slice: x: 2, y: 2, z: 4, core: 2. Of those that a mesh axis runs over, the one named last changes fastest.
Arguments:
- maps: bfloat16 [8, 4096, 4096], P('grp', 'theta', 'phi'), parts along dimension 0, may hold values from -6 to 6
- deltas: bfloat16 [4096, 4, 4096], P('phi', None, 'theta'), may hold values from -1 to 1
- spin_rows: bfloat16 [4096, 2, 4], P('phi'), may hold values from -1 to 1
- ell_index: int32 [4], replicated, may hold values from 1024 to 2047
- owner_map: int32 [4096], replicated, may hold values from 0 to 4095, each once
- prior: float32 [4], replicated, may hold values from 0.3 to 3
Outputs:
- gradient: float32 [8, 2, 4096], P('grp', None, ('theta', 'phi')), parts along dimension 0
There are 2 independent parts, one for each index of `grp`. A program takes and returns all parts, laid end to end along the dimension named above; an argument that names none is the same for every part. Nothing has to cross between parts.
Inputs may be any that keep to these rules, and one draw needn't show every extreme that they name: `ell_index`: every selected degree is at least 1024; tables may repeat a degree. A permutation of the Fourier indices; slot s of deltas and of the output belongs to the frequency owner_map[s].
All inputs are finite; a program needn't handle non-finite values.
Results may differ from a plain program's by a relative error of at most 0.0003.
Values may be sent and summed in bfloat16 or wider, within the bound.
A program may use at most 256 MiB of HBM per device.

v0:
```python
import functools
import math

import jax
import jax.numpy as jnp
from jax import lax
from jax.experimental import pallas as pl
from jax.experimental.pallas import tpu as pltpu
from jax.sharding import PartitionSpec as P


def exact_einsum(form, table, operand):
    return jnp.einsum(form, table, operand, precision=lax.Precision.HIGHEST)


def angle_tables(row_count, start, count, modulus):
    freq_rows = jnp.arange(row_count, dtype=jnp.int32)
    sample_cols = start + jnp.arange(count, dtype=jnp.int32)
    angles = (
        2.0
        * math.pi
        / modulus
        * jnp.mod(freq_rows[:, None] * sample_cols[None, :], modulus).astype(jnp.float32)
    )
    return (jnp.cos(angles), jnp.sin(angles))


def row_transform(real_part, imag_part, outer_len, inner_len):
    row_count = real_part.shape[0]
    length = outer_len * inner_len
    cos_a, sin_a = angle_tables(outer_len, 0, outer_len, outer_len)
    real_blocks = real_part.reshape(row_count, outer_len, inner_len)
    section_real = exact_einsum("ka,rab->rkb", cos_a, real_blocks)
    section_imag = -exact_einsum("ka,rab->rkb", sin_a, real_blocks)
    if imag_part is not None:
        imag_blocks = imag_part.reshape(row_count, outer_len, inner_len)
        section_real = section_real + exact_einsum("ka,rab->rkb", sin_a, imag_blocks)
        section_imag = section_imag + exact_einsum("ka,rab->rkb", cos_a, imag_blocks)
    cos_t, sin_t = angle_tables(outer_len, 0, inner_len, length)
    turned_real = section_real * cos_t + section_imag * sin_t
    turned_imag = section_imag * cos_t - section_real * sin_t
    cos_b, sin_b = angle_tables(inner_len, 0, inner_len, inner_len)
    out_real = exact_einsum("qb,rkb->rqk", cos_b, turned_real) + exact_einsum(
        "qb,rkb->rqk", sin_b, turned_imag
    )
    out_imag = exact_einsum("qb,rkb->rqk", cos_b, turned_imag) - exact_einsum(
        "qb,rkb->rqk", sin_b, turned_real
    )
    return (out_real.reshape(row_count, length), out_imag.reshape(row_count, length))


def column_transform(real_part, imag_part, outer_len, inner_len, start):
    fields = real_part.shape[0]
    count = real_part.shape[2]
    slots = real_part.shape[3]
    length = outer_len * inner_len
    cos_a, sin_a = angle_tables(outer_len, 0, outer_len, outer_len)
    section_real = exact_einsum("ka,fabm->fkbm", cos_a, real_part) + exact_einsum(
        "ka,fabm->fkbm", sin_a, imag_part
    )
    section_imag = exact_einsum("ka,fabm->fkbm", cos_a, imag_part) - exact_einsum(
        "ka,fabm->fkbm", sin_a, real_part
    )
    cos_t, sin_t = angle_tables(outer_len, start, count, length)
    cos_t = cos_t[:, :, None]
    sin_t = sin_t[:, :, None]
    turned_real = section_real * cos_t + section_imag * sin_t
    turned_imag = section_imag * cos_t - section_real * sin_t
    cos_b, sin_b = angle_tables(inner_len, start, count, inner_len)
    out_real = exact_einsum("qb,fkbm->fqkm", cos_b, turned_real) + exact_einsum(
        "qb,fkbm->fqkm", sin_b, turned_imag
    )
    out_imag = exact_einsum("qb,fkbm->fqkm", cos_b, turned_imag) - exact_einsum(
        "qb,fkbm->fqkm", sin_b, turned_real
    )
    return (out_real.reshape(fields, length, slots), out_imag.reshape(fields, length, slots))


def accumulate(spectrum_block, table_block, spin_block, length, ell_index):
    count = table_block.shape[0]
    positions = jnp.arange(count, dtype=jnp.int32)
    freq = jnp.where(positions < length // 2, positions, positions - length)
    terms = []
    for degree in range(table_block.shape[1]):
        keep_rows = (jnp.abs(freq) <= ell_index[degree]).astype(jnp.float32)
        row_weights = spin_block[:, :, degree].astype(jnp.float32).T * keep_rows[None, :]
        table = table_block[:, degree, :].astype(jnp.float32)
        terms.append(
            jnp.einsum(
                "fk,ks,xfks->fxs",
                row_weights,
                table,
                spectrum_block,
                precision=lax.Precision.HIGHEST,
            )
        )
    return jnp.stack(terms)


def on_device_general(maps, deltas, spin_rows, ell_index, owner_map, prior):
    theta_count = lax.axis_size("theta")
    phi_count = lax.axis_size("phi")
    length = maps.shape[2] * phi_count
    values = maps.astype(jnp.float32)
    planes = jnp.stack([values[0], values[1] * values[2], values[1] * values[3]])
    row_planes = lax.all_to_all(planes, "phi", split_axis=1, concat_axis=2, tiled=True)
    inner_len = length // theta_count
    spectra = [
        row_transform(row_planes[0], None, theta_count, inner_len),
        row_transform(row_planes[1], row_planes[2], theta_count, inner_len),
    ]
    stacked = jnp.stack(
        [
            jnp.stack([spectrum[0] for spectrum in spectra]),
            jnp.stack([spectrum[1] for spectrum in spectra]),
        ]
    )
    permuted = jnp.take(stacked, owner_map, axis=3)
    columns = lax.all_to_all(permuted, "theta", split_axis=3, concat_axis=2, tiled=True)
    fields = columns.shape[1]
    slots = columns.shape[3]
    sub_rows = columns.shape[2] // theta_count
    blocks = columns.reshape(2, fields, theta_count, sub_rows, slots)
    row_start = lax.axis_index("phi") * sub_rows
    spec_real, spec_imag = column_transform(blocks[0], blocks[1], theta_count, inner_len, row_start)
    combined = jnp.stack([spec_real, spec_imag])
    totals = accumulate(
        combined,
        lax.all_gather(deltas, "phi", axis=0, tiled=True),
        lax.all_gather(spin_rows, "phi", axis=0, tiled=True),
        length,
        ell_index,
    )
    shares = lax.psum_scatter(totals, "phi", scatter_dimension=3, tiled=True)
    share_count = shares.shape[3]
    slot_start = lax.axis_index("theta") * slots + lax.axis_index("phi") * share_count
    share_ids = lax.dynamic_slice_in_dim(owner_map, slot_start, share_count)
    slot_freq = jnp.where(share_ids < length // 2, share_ids, share_ids - length)
    ell_float = ell_index.astype(jnp.float32)
    weight = 2.0 * math.pi / length * jnp.sqrt((2.0 * ell_float + 1.0) / (4.0 * math.pi)) / length
    keep_slots = (jnp.abs(slot_freq)[None, :] <= ell_index[:, None]).astype(jnp.float32) * weight[
        :, None
    ]
    scalar_real = shares[:, 0, 0] * keep_slots
    scalar_imag = shares[:, 0, 1] * keep_slots
    spin_real = shares[:, 1, 0] * keep_slots
    spin_imag = shares[:, 1, 1] * keep_slots
    coupling = (prior * jnp.sqrt(ell_float * (ell_float + 1.0)) / (length // 2))[:, None]
    inner_real = -spin_imag - coupling * scalar_real
    inner_imag = spin_real - coupling * scalar_imag
    turns = jnp.mod(-slot_freq, 4)
    phase_real = jnp.where(turns == 0, 1.0, jnp.where(turns == 2, -1.0, 0.0)).astype(jnp.float32)[
        None, :
    ]
    phase_imag = jnp.where(turns == 1, 1.0, jnp.where(turns == 3, -1.0, 0.0)).astype(jnp.float32)[
        None, :
    ]
    out_real = phase_real * inner_real - phase_imag * inner_imag
    out_imag = phase_real * inner_imag + phase_imag * inner_real
    return jnp.stack([out_real, out_imag], axis=1)


ROW_OUTER = 8
VMEM_LIMIT = 60 * 1024 * 1024
CODE_TOP = 32767.0


def cplx_add(x, y):
    return tuple(b if a is None else a if b is None else a + b for a, b in zip(x, y))


def cplx_sub(x, y):
    return tuple(
        (None if b is None else -b) if a is None else a if b is None else a - b
        for a, b in zip(x, y)
    )


def turn(x, step, count):
    real, imag = x
    if step == 0:
        return x
    if 4 * step == count:
        return (imag, None if real is None else -real)
    cos_v = math.cos(2.0 * math.pi * step / count)
    sin_v = math.sin(2.0 * math.pi * step / count)
    if imag is None:
        return (real * cos_v, real * -sin_v)
    if 8 * step == count:
        return ((real + imag) * cos_v, (imag - real) * cos_v)
    if 8 * step == 3 * count:
        return ((imag - real) * sin_v, (real + imag) * -sin_v)
    return (real * cos_v + imag * sin_v, imag * cos_v - real * sin_v)


def butterfly(items):
    count = len(items)
    if count == 1:
        return items
    even, odd = butterfly(items[::2]), butterfly(items[1::2])
    turned = [turn(x, step, count) for step, x in enumerate(odd)]
    return [cplx_add(a, b) for a, b in zip(even, turned)] + [
        cplx_sub(a, b) for a, b in zip(even, turned)
    ]


def split_store(high, low, where, value):
    top = value.astype(jnp.bfloat16)
    high[where] = top
    low[where] = (value - top.astype(jnp.float32)).astype(jnp.bfloat16)


def store_matrix(cos_ref, sin_ref, high, low):
    size = cos_ref.shape[0]
    first, second = slice(0, size), slice(size, 2 * size)
    cos_v, sin_v = cos_ref[...], sin_ref[...]
    split_store(high, low, (first, first), cos_v)
    split_store(high, low, (first, second), sin_v)
    split_store(high, low, (second, first), -sin_v)
    split_store(high, low, (second, second), cos_v)


def store_turned(high, low, k, rows, item, cos_t, sin_t):
    real, imag = item
    size = real.shape[1]
    cos_k, sin_k = cos_t[k : k + 1, :], sin_t[k : k + 1, :]
    if imag is None:
        out_real, out_imag = real * cos_k, real * -sin_k
    else:
        out_real, out_imag = real * cos_k + imag * sin_k, imag * cos_k - real * sin_k
    split_store(high, low, (k, rows, slice(0, size)), out_real)
    split_store(high, low, (k, rows, slice(size, 2 * size)), out_imag)


def dot_nt(left, right):
    return lax.dot_general(
        left, right, (((1,), (1,)), ((), ())), preferred_element_type=jnp.float32
    )


def three_dots(mat_high, mat_low, x_high, x_low, k):
    high = x_high[k]
    return (
        dot_nt(mat_high[...], high) + dot_nt(mat_high[...], x_low[k]) + dot_nt(mat_low[...], high)
    )


def row_kernel(kept, *refs):
    planes = refs[:-10]
    cos_b, sin_b, cos_t, sin_t, code_ref, scale_ref, mat_high, mat_low, x_high, x_low = refs[-10:]
    k = pl.program_id(0)
    inner = cos_b.shape[0]

    @pl.when(k == 0)
    def _():
        store_matrix(cos_b, sin_b, mat_high, mat_low)
        step_rows = 16

        def chunk(step, carry):
            rows = pl.ds(pl.multiple_of(step * step_rows, step_rows), step_rows)

            def part(ref, a):
                return ref[0, rows, a * inner : (a + 1) * inner].astype(jnp.float32)

            items = []
            for a in range(ROW_OUTER):
                if len(planes) == 1:
                    items.append((part(planes[0], a), None))
                else:
                    base = part(planes[0], a)
                    items.append((base * part(planes[1], a), base * part(planes[2], a)))
            done = butterfly(items)
            for out in range(kept):
                store_turned(x_high, x_low, out, rows, done[out], cos_t, sin_t)
            return carry

        lax.fori_loop(0, planes[0].shape[1] // step_rows, chunk, 0)

    both = three_dots(mat_high, mat_low, x_high, x_low, k)
    real, imag = both[:inner], both[inner:]
    top = jnp.max(jnp.maximum(jnp.abs(real), jnp.abs(imag)), axis=1, keepdims=True)
    top = jnp.maximum(top, 1e-30)
    factor = CODE_TOP / top
    code_real = jnp.round(real * factor).astype(jnp.int32)
    code_imag = jnp.round(imag * factor).astype(jnp.int32)
    code_ref[0] = (code_real << 16) | (code_imag & 0xFFFF)
    scale_ref[0] = jnp.broadcast_to(top * (1.0 / CODE_TOP), (inner, 128))


def row_call(maps, places, kept, cos_b, sin_b, cos_t, sin_t):
    rows, length = maps.shape[1:]
    inner = cos_b.shape[0]
    whole = lambda shape: pl.BlockSpec(shape, lambda k: (0, 0))
    plane = lambda place: pl.BlockSpec((1, rows, length), lambda k: (place, 0, 0))
    return pl.pallas_call(
        functools.partial(row_kernel, kept),
        grid=(kept,),
        in_specs=[plane(place) for place in places]
        + [whole(cos_b.shape), whole(sin_b.shape), whole(cos_t.shape), whole(sin_t.shape)],
        out_specs=[
            pl.BlockSpec((1, inner, rows), lambda k: (k, 0, 0)),
            pl.BlockSpec((1, inner, 128), lambda k: (k, 0, 0)),
        ],
        out_shape=[
            jax.ShapeDtypeStruct((kept, inner, rows), jnp.int32),
            jax.ShapeDtypeStruct((kept, inner, 128), jnp.float32),
        ],
        scratch_shapes=[
            pltpu.VMEM((2 * inner, 2 * inner), jnp.bfloat16),
            pltpu.VMEM((2 * inner, 2 * inner), jnp.bfloat16),
            pltpu.VMEM((kept, rows, 2 * inner), jnp.bfloat16),
            pltpu.VMEM((kept, rows, 2 * inner), jnp.bfloat16),
        ],
        compiler_params=pltpu.CompilerParams(vmem_limit_bytes=VMEM_LIMIT),
        cost_estimate=pl.CostEstimate(
            flops=24 * kept * inner * inner * rows,
            bytes_accessed=len(places) * rows * length * 2 + kept * inner * (rows + 128) * 4,
            transcendentals=0,
        ),
    )(*([maps] * len(places)), cos_b, sin_b, cos_t, sin_t)


def column_kernel(
    code_ref, sre_ref, sim_ref, table_ref, row_w, cos_b, sin_b, cos_t, sin_t, out_ref,
    mat_high, mat_low, x_high, x_low, total,
):
    k = pl.program_id(0)
    outer = code_ref.shape[0]
    slots = code_ref.shape[1]
    inner = code_ref.shape[2]
    degrees = table_ref.shape[1]

    @pl.when(k == 0)
    def _():
        store_matrix(cos_b, sin_b, mat_high, mat_low)
        total[...] = jnp.zeros_like(total)
        step_rows = 16

        def chunk(step, carry):
            rows = pl.ds(pl.multiple_of(step * step_rows, step_rows), step_rows)
            sre, sim = sre_ref[rows, :], sim_ref[rows, :]
            items = []
            for a in range(outer):
                code = code_ref[a, rows, :]
                real = (code >> 16).astype(jnp.float32) * sre[:, a : a + 1]
                imag = ((code << 16) >> 16).astype(jnp.float32) * sim[:, a : a + 1]
                items.append((real, imag))
            for out, item in enumerate(butterfly(items)):
                store_turned(x_high, x_low, out, rows, item, cos_t, sin_t)
            return carry

        lax.fori_loop(0, slots // step_rows, chunk, 0)

    both = three_dots(mat_high, mat_low, x_high, x_low, k)
    real, imag = both[:inner], both[inner:]
    for degree in range(degrees):
        weighted = table_ref[0, degree].astype(jnp.float32) * row_w[0, :, degree : degree + 1]
        for part, value in enumerate((real, imag)):
            total[2 * degree + part] += jnp.sum(
                (weighted * value).reshape(inner // 8, 8, slots), axis=0
            )

    @pl.when(k == outer - 1)
    def _():
        out_ref[...] = jnp.sum(total[...], axis=1)


def column_call(codes, sre, sim, tables, row_w, cos_b, sin_b, cos_t, sin_t):
    outer, slots, inner = codes.shape
    degrees = tables.shape[1]
    whole = lambda shape: pl.BlockSpec(shape, lambda k: (0,) * len(shape))
    return pl.pallas_call(
        column_kernel,
        grid=(outer,),
        in_specs=[
            whole(codes.shape),
            whole(sre.shape),
            whole(sim.shape),
            pl.BlockSpec((1, degrees, inner, slots), lambda k: (k, 0, 0, 0)),
            pl.BlockSpec((1, inner, degrees), lambda k: (k, 0, 0)),
            whole(cos_b.shape),
            whole(sin_b.shape),
            whole(cos_t.shape),
            whole(sin_t.shape),
        ],
        out_specs=whole((2 * degrees, slots)),
        out_shape=jax.ShapeDtypeStruct((2 * degrees, slots), jnp.float32),
        scratch_shapes=[
            pltpu.VMEM((2 * inner, 2 * inner), jnp.bfloat16),
            pltpu.VMEM((2 * inner, 2 * inner), jnp.bfloat16),
            pltpu.VMEM((outer, slots, 2 * inner), jnp.bfloat16),
            pltpu.VMEM((outer, slots, 2 * inner), jnp.bfloat16),
            pltpu.VMEM((2 * degrees, 8, slots), jnp.float32),
        ],
        compiler_params=pltpu.CompilerParams(vmem_limit_bytes=VMEM_LIMIT),
        cost_estimate=pl.CostEstimate(
            flops=24 * outer * inner * inner * slots,
            bytes_accessed=outer * slots * inner * (4 + 2 * degrees),
            transcendentals=0,
        ),
    )(codes, sre, sim, tables, row_w, cos_b, sin_b, cos_t, sin_t)


def trig_tables(row_ids, col_ids, modulus):
    product = jnp.mod(row_ids[:, None] * col_ids[None, :], modulus)
    angles = (2.0 * math.pi / modulus) * product.astype(jnp.float32)
    return jnp.cos(angles), jnp.sin(angles)


def signed(ids, length):
    return jnp.where(ids < length // 2, ids, ids - length)


def on_device(maps, deltas, spin_rows, ell_index, owner_map, prior):
    owners = ("theta", "phi")
    phi_count = lax.axis_size("phi")
    length = maps.shape[2] * phi_count
    outer = lax.axis_size("theta") * phi_count
    sub_rows = length // outer
    slots = sub_rows
    row_inner = length // ROW_OUTER
    ids = lax.optimization_barrier(jnp.arange(length, dtype=jnp.int32))
    row_trig = trig_tables(ids[:row_inner], ids[:row_inner], row_inner) + trig_tables(
        ids[:ROW_OUTER], ids[:row_inner], length
    )
    col_trig = trig_tables(ids[:sub_rows], ids[:sub_rows], sub_rows) + trig_tables(
        ids[:outer], ids[:sub_rows], length
    )
    rows = lax.all_to_all(maps, "phi", split_axis=1, concat_axis=2, tiled=True)

    residue = owner_map % ROW_OUTER
    flipped = residue > ROW_OUTER // 2
    half_map = jnp.where(flipped, length - owner_map, owner_map)
    slot_start = (lax.axis_index("theta") * phi_count + lax.axis_index("phi")) * slots
    own = lambda array: lax.dynamic_slice_in_dim(array, slot_start, slots)
    own_ids = own(owner_map)

    def spectrum(places, kept, freq):
        codes, scales = row_call(rows, places, kept, *row_trig)
        place = (freq % ROW_OUTER) * row_inner + freq // ROW_OUTER
        table = codes.reshape(kept * row_inner, sub_rows)
        sorted_codes = table.at[place].get(mode="promise_in_bounds", unique_indices=False)
        received = lax.all_to_all(
            sorted_codes.reshape(outer, slots, sub_rows), owners, 0, 0, tiled=True
        )
        flat = lax.all_gather(scales[:, :, 0].reshape(-1), owners, axis=0)
        picks = (own(place)[:, None] == ids[None, : kept * row_inner]).astype(jnp.float32)
        own_scales = jnp.einsum("am,sm->sa", flat, picks, precision=lax.Precision.HIGHEST)
        return received, own_scales

    code_scalar, scale_scalar = spectrum((0,), ROW_OUTER // 2 + 1, half_map)
    code_spin, scale_spin = spectrum((1, 2, 3), ROW_OUTER, owner_map)

    tables = lax.all_to_all(deltas, "phi", split_axis=2, concat_axis=0, tiled=True)
    degrees = tables.shape[1]
    tables = tables.reshape(sub_rows, outer, degrees, slots).transpose(1, 2, 0, 3)
    spins = lax.all_gather(spin_rows, "phi", axis=0, tiled=True).astype(jnp.float32)
    keep_rows = jnp.abs(signed(ids, length))[:, None] <= ell_index[None, :]
    row_w = jnp.where(keep_rows[:, None, :], spins, 0.0)
    row_w = row_w.reshape(sub_rows, outer, 2, degrees).transpose(2, 1, 0, 3)

    mirror = jnp.where(own(flipped), -1.0, 1.0)[:, None]
    scalar = column_call(
        code_scalar, scale_scalar, scale_scalar * mirror, tables, row_w[0], *col_trig
    ).reshape(degrees, 2, slots)
    spin = column_call(
        code_spin, scale_spin, scale_spin, tables, row_w[1], *col_trig
    ).reshape(degrees, 2, slots)

    slot_freq = signed(own_ids, length)
    ell_float = ell_index.astype(jnp.float32)
    weight = 2.0 * math.pi / length * jnp.sqrt((2.0 * ell_float + 1.0) / (4.0 * math.pi)) / length
    keep = jnp.abs(slot_freq)[None, :] <= ell_index[:, None]
    keep_slots = keep.astype(jnp.float32) * weight[:, None]
    coupling = (prior * jnp.sqrt(ell_float * (ell_float + 1.0)) / (length // 2))[:, None]
    inner_real = (-spin[:, 1] - coupling * scalar[:, 0]) * keep_slots
    inner_imag = (spin[:, 0] - coupling * scalar[:, 1]) * keep_slots
    turns = jnp.mod(-slot_freq, 4)[None, :]
    phase_real = jnp.where(turns == 0, 1.0, jnp.where(turns == 2, -1.0, 0.0))
    phase_imag = jnp.where(turns == 1, 1.0, jnp.where(turns == 3, -1.0, 0.0))
    out_real = phase_real * inner_real - phase_imag * inner_imag
    out_imag = phase_real * inner_imag + phase_imag * inner_real
    return jnp.stack([out_real, out_imag], axis=1)


def solution(mesh):
    owner_count = mesh.shape["theta"] * mesh.shape["phi"]
    body = on_device if owner_count <= 16 else on_device_general
    placed = (
        P("grp", "theta", "phi"),
        P("phi", None, "theta"),
        P("phi", None, None),
        P(),
        P(),
        P(),
    )
    return jax.shard_map(
        body,
        mesh=mesh,
        in_specs=placed,
        out_specs=P("grp", None, ("theta", "phi")),
        check_vma=False,
    )
```

profile of v0, /device:TPU:0, one launch (start us, length us, event | category | flops | bytes accessed | tf_op | source)
XLA Modules:
  0.0 413.2 jit_solution(10530586881696997783)
XLA Ops:
  0.0 12.2 %copy.39 = bf16[4,512,2048]{2,0,1:T(4,128)(2,1)} copy(bf16[4,512,2048]{2,1,0:T(8,128)(2,1)} %param.6) | data formatting | bytes 16777216 | tf_op args[0]
  12.2 7.1 %all-to-all-start = ((bf16[4,512,2048]{2,0,1:T(4,128)(2,1)}), bf16[4,512,2048]{2,0,1:T(4,128)(2,1)}, u32[]{:S(2)}, u32[]{:S(2)}) async-start(bf16[4,512,2048]{2,0,1:T(4,128)(2,1)} %copy.39), calls=%async_computation | async-start | bytes 16777216 | tf_op jit(solution)/shard_map/all_to_all | solution.py:429
  19.4 5.9 %fusion.11 = (f32[512,512]{1,0:T(8,128)}, f32[512,512]{1,0:T(8,128)}) fusion(s32[512]{0:T(512)S(1)} %slice.60), kind=kLoop, calls=%fused_computation.24 | loop fusion | flops 3670016 | bytes 2099200 | tf_op jit(solution)/shard_map/sin | solution.py:407
  26.1 19.0 %copy.41 = bf16[2048,4,512]{0,1,2:T(4,128)(2,1)} copy(bf16[2048,4,512]{2,1,0:T(4,128)(2,1)} %param.7) | data formatting | bytes 16777216 | tf_op args[1]
  45.1 6.9 %all-to-all-start.2 = ((bf16[2048,4,512]{0,1,2:T(4,128)(2,1)}), bf16[2048,4,512]{0,1,2:T(4,128)(2,1)}, u32[]{:S(2)}, u32[]{:S(2)}) async-start(bf16[2048,4,512]{0,1,2:T(4,128)(2,1)} %copy.41), calls=%async_computation.2 | async-start | bytes 16777216 | tf_op jit(solution)/shard_map/all_to_all | solution.py:454
  52.0 16.4 %copy.68 = bf16[4,2,256,2048]{3,1,2,0:T(2,128)(2,1)} copy(bf16[4,2,256,2048]{3,0,2,1:T(4,128)(2,1)} %bitcast) | data formatting | bytes 16777216 | tf_op jit(solution)/shard_map/all_to_all | solution.py:429
  68.5 14.5 %all_to_all.33.refs_0_.refs_1_.refs_2_ = bf16[4,256,4096]{2,1,0:T(8,128)(2,1)} reshape(bf16[4,256,2,2048]{3,2,1,0:T(2,128)(2,1)} %bitcast.32) | data formatting | bytes 16777216 | tf_op jit(solution)/shard_map/all_to_all | solution.py:429
  83.0 24.5 %shard_map.64 = (s32[8,512,256]{2,1,0:T(8,128)}, f32[8,512,128]{2,1,0:T(8,128)}) custom-call(bf16[4,256,4096]{2,1,0:T(8,128)(2,1)} %all_to_all.33.refs_0_.refs_1_.refs_2_, bf16[4,256,4096]{2,1,0:T(8,128)(2,1)} %all_to_all.33.refs_0_.refs_1_.refs_2_, bf16[4,256,4096]{2,1,0:T(8,128)(2,1)} %all_to_all.33.refs_0_.refs_1_.refs_2_, ...), custom_call_target="tpu_custom_call" | custom-call | flops 12884901888 | bytes 12582912 | tf_op jit(solution)/shard_map/pallas_call | solution.py:295
  107.5 18.3 %gather_fusion = s32[4096,256]{1,0:T(8,128)} fusion(s32[4096,256]{1,0:T(8,128)} %bitcast.31, s32[4096]{0:T(1024)S(1)} %get-tuple-element.18), kind=kCustom, calls=%fused_computation | custom fusion | bytes 8404992 | tf_op jit(solution)/shard_map/gather | solution.py:442
  125.8 7.6 %all-to-all-start.1 = ((s32[16,256,256]{2,1,0:T(8,128)}), s32[16,256,256]{2,1,0:T(8,128)}, u32[]{:S(2)}, u32[]{:S(2)}) async-start(s32[16,256,256]{2,1,0:T(8,128)} %bitcast.36), calls=%async_computation.1 | async-start | bytes 8388608 | tf_op jit(solution)/shard_map/all_to_all | solution.py:443
  133.4 15.3 %shard_map.66 = (s32[5,512,256]{2,1,0:T(8,128)}, f32[5,512,128]{2,1,0:T(8,128)}) custom-call(bf16[4,256,4096]{2,1,0:T(8,128)(2,1)} %all_to_all.33.refs_0_.refs_1_.refs_2_, f32[512,512]{1,0:T(8,128)} %get-tuple-element.29.refs_3_.refs_1_, f32[512,512]{1,0:T(8,128)} %get-tuple-element.28.refs_4_.refs_2_, f32[8,512]{1,0:T(8,128)} %get-tuple-element.27.refs_5_.refs_3_, ...), custom_call_target="tpu_custom_call" | custom-call | flops 8053063680 | bytes 6029312 | tf_op jit(solution)/shard_map/pallas_call | solution.py:295
  148.7 17.9 %gather_fusion.1 = s32[4096,256]{1,0:T(8,128)} fusion(s32[2560,256]{1,0:T(8,128)} %bitcast.30, s32[4096]{0:T(1024)S(1)} %get-tuple-element.24), kind=kCustom, calls=%fused_computation.1 | custom fusion | bytes 8404992 | tf_op jit(solution)/shard_map/gather | solution.py:442
  166.6 44.3 %all-to-all-done.1.code_ref = s32[16,256,256]{2,1,0:T(8,128)} async-done(((s32[16,256,256]{2,1,0:T(8,128)}), s32[16,256,256]{2,1,0:T(8,128)}, u32[]{:S(2)}, u32[]{:S(2)}) %all-to-all-start.1) | async-done | bytes 4194336 | tf_op jit(solution)/shard_map/all_to_all | solution.py:443
  210.9 19.8 %all-to-all-start.3 = ((s32[16,256,256]{2,1,0:T(8,128)}), s32[16,256,256]{2,1,0:T(8,128)}, u32[]{:S(2)}, u32[]{:S(2)}) async-start(s32[16,256,256]{2,1,0:T(8,128)} %bitcast.35), calls=%async_computation.3 | async-start | bytes 8388608 | tf_op jit(solution)/shard_map/all_to_all | solution.py:443
  233.6 5.0 %copy.45 = f32[256,16,2,4]{3,0,1,2:T(8,128)} copy(f32[256,16,2,4]{1,0,3,2:T(8,128)S(1)} %reshape.180) | data formatting | bytes 262144 | tf_op jit(solution)/shard_map/reshape | solution.py:460
  241.0 11.2 %copy.42 = bf16[2048,4,512]{0,2,1:T(8,128)(2,1)} copy(bf16[2048,4,512]{0,1,2:T(4,128)(2,1)} %all-to-all-done.2) | data formatting | bytes 16777216 | tf_op jit(solution)/shard_map/all_to_all | solution.py:454
  252.3 11.4 %copy.43 = bf16[2,2048,4,256]{3,1,0,2:T(8,128)(2,1)} copy(bf16[2,2048,4,256]{1,3,0,2:T(8,128)(2,1)} %bitcast.33) | data formatting | bytes 16777216 | tf_op jit(solution)/shard_map/all_to_all | solution.py:454
  263.7 9.7 %copy.67 = bf16[256,16,4,256]{3,0,2,1:T(8,128)(2,1)} copy(bf16[256,16,4,256]{3,1,0,2:T(8,128)(2,1)} %bitcast.34) | data formatting | bytes 16777216 | tf_op jit(solution)/shard_map/reshape | solution.py:456
  273.4 44.9 %all-gather.1 = f32[16,1,2560]{2,1,0:T(1,128)S(1)} all-gather(f32[1,1,2560]{2,1,0:T(1,128)S(1)} %reshape.205), channel_id=1, replica_groups=mesh['grp'=2,'theta'=8,'phi'=2] {'theta','phi'}, dimensions={0}, use_global_device_ids=true | all-gather | bytes 174080 | tf_op jit(solution)/shard_map/all_gather | solution.py:446
  318.6 36.1 %all-gather = f32[16,1,4096]{2,1,0:T(1,128)S(1)} all-gather(f32[1,1,4096]{2,1,0:T(1,128)S(1)} %reshape.203), channel_id=1, replica_groups=mesh['grp'=2,'theta'=8,'phi'=2] {'theta','phi'}, dimensions={0}, use_global_device_ids=true | all-gather | bytes 278528 | tf_op jit(solution)/shard_map/all_gather | solution.py:446
  355.6 2.6 fusion.sre_ref.sim_ref
  362.0 2.3 slice_bitcast_fusion.1
  364.3 23.4 %shard_map.65 = f32[8,256]{1,0:T(8,128)} custom-call(s32[16,256,256]{2,1,0:T(8,128)} %all-to-all-done.1.code_ref, f32[256,16]{1,0:T(8,128)} %fusion.sre_ref.sim_ref, f32[256,16]{1,0:T(8,128)} %fusion.sre_ref.sim_ref, bf16[16,4,256,256]{3,2,1,0:T(8,128)(2,1)} %bitcast.38, f32[16,256,4]{2,1,0:T(8,128)} %get-tuple-element.22.row_w, ...), custom_call_target="tpu_custom_call" | custom-call | flops 6442450944 | bytes 12582912 | tf_op jit(solution)/shard_map/pallas_call | solution.py:372
  388.4 23.3 %shard_map.67 = f32[8,256]{1,0:T(8,128)} custom-call(s32[16,256,256]{2,1,0:T(8,128)} %all-to-all-done.3.code_ref, f32[256,16]{1,0:T(8,128)} %get-tuple-element.37.sre_ref, f32[256,16]{1,0:T(8,128)} %get-tuple-element.36.sim_ref, bf16[16,4,256,256]{3,2,1,0:T(8,128)(2,1)} %bitcast.39, f32[16,256,4]{2,1,0:T(8,128)} %get-tuple-element.23.row_w, ...), custom_call_target="tpu_custom_call" | custom-call | flops 6442450944 | bytes 12582912 | tf_op jit(solution)/shard_map/pallas_call | solution.py:372
  (54 shorter events, 13.1 us)
Async XLA Ops:
  12.2 13.8 %copy-start.4 = (s32[4096]{0:T(1024)S(1)}, s32[4096]{0:T(1024)}, u32[]{:S(2)}) copy-start(s32[4096]{0:T(1024)} %param.10) | copy-start | bytes 49156
  12.2 32.9 %all-to-all-start = ((bf16[4,512,2048]{2,0,1:T(4,128)(2,1)}), bf16[4,512,2048]{2,0,1:T(4,128)(2,1)}, u32[]{:S(2)}, u32[]{:S(2)}) async-start(bf16[4,512,2048]{2,0,1:T(4,128)(2,1)} %copy.39), calls=%async_computation | async-start | bytes 16777216 | tf_op jit(solution)/shard_map/all_to_all | solution.py:429
  19.4 213.7 %copy-start.2 = (s32[4096]{0:T(1024)}, s32[4096]{0:T(1024)S(1)}, u32[]{:S(2)}) copy-start(s32[4096]{0:T(1024)S(1)} %iota.3) | copy-start | bytes 49156
  45.1 80.7 %all-to-all-start.2 = ((bf16[2048,4,512]{0,1,2:T(4,128)(2,1)}), bf16[2048,4,512]{0,1,2:T(4,128)(2,1)}, u32[]{:S(2)}, u32[]{:S(2)}) async-start(bf16[2048,4,512]{0,1,2:T(4,128)(2,1)} %copy.41), calls=%async_computation.2 | async-start | bytes 16777216 | tf_op jit(solution)/shard_map/all_to_all | solution.py:454
  125.8 85.1 %all-to-all-start.1 = ((s32[16,256,256]{2,1,0:T(8,128)}), s32[16,256,256]{2,1,0:T(8,128)}, u32[]{:S(2)}, u32[]{:S(2)}) async-start(s32[16,256,256]{2,1,0:T(8,128)} %bitcast.36), calls=%async_computation.1 | async-start | bytes 8388608 | tf_op jit(solution)/shard_map/all_to_all | solution.py:443
  210.9 20.0 %copy-start.5 = (bf16[2048,2,4]{0,2,1:T(4,128)(2,1)S(1)}, bf16[2048,2,4]{0,2,1:T(4,128)(2,1)}, u32[]{:S(2)}) copy-start(bf16[2048,2,4]{0,2,1:T(4,128)(2,1)} %param.8) | copy-start | bytes 98308
  210.9 22.2 %copy-start.6 = (s32[4]{0:T(128)S(1)}, s32[4]{0:T(128)}, u32[]{:S(2)}) copy-start(s32[4]{0:T(128)} %param.9) | copy-start | bytes 52
  210.9 177.5 %all-to-all-start.3 = ((s32[16,256,256]{2,1,0:T(8,128)}), s32[16,256,256]{2,1,0:T(8,128)}, u32[]{:S(2)}, u32[]{:S(2)}) async-start(s32[16,256,256]{2,1,0:T(8,128)} %bitcast.35), calls=%async_computation.3 | async-start | bytes 8388608 | tf_op jit(solution)/shard_map/all_to_all | solution.py:443
  230.7 9.6 %copy-start.1 = (f32[8,512,128]{2,1,0:T(8,128)S(1)}, f32[8,512,128]{2,1,0:T(8,128)}, u32[]{:S(2)}) copy-start(f32[8,512,128]{2,1,0:T(8,128)} %get-tuple-element.10) | copy-start | bytes 6291460
  263.7 91.0 %copy-start.7 = (f32[4]{0:T(128)S(1)}, f32[4]{0:T(128)}, u32[]{:S(2)}) copy-start(f32[4]{0:T(128)} %param.11) | copy-start | bytes 52
  263.7 91.1 %slice-start = ((s32[4096]{0:T(1024)}), s32[16]{0:T(128)S(1)}, s32[]{:S(2)}) async-start(s32[4096]{0:T(1024)} %copy-done.2), calls=%async_computation.4 | async-start | bytes 1024 | tf_op jit(solution)/shard_map/slice | solution.py:427
  263.7 91.8 %copy-start.3 = (s32[4096]{0:T(1024)S(1)}, s32[4096]{0:T(1024)}, u32[]{:S(2)}) copy-start(s32[4096]{0:T(1024)} %copy-done.2) | copy-start | bytes 49156
  263.7 94.4 %slice-start.1 = ((s32[4096]{0:T(1024)}), s32[2560]{0:T(1024)S(1)}, s32[]{:S(2)}) async-start(s32[4096]{0:T(1024)} %copy-done.2), calls=%async_computation.5 | async-start | bytes 24576 | tf_op jit(solution)/shard_map/slice | solution.py:447
  273.4 88.6 %copy-start = (f32[256,16,2,4]{3,0,1,2:T(8,128)S(1)}, f32[256,16,2,4]{3,0,1,2:T(8,128)}, u32[]{:S(2)}) copy-start(f32[256,16,2,4]{3,0,1,2:T(8,128)} %copy.45) | copy-start | bytes 393220
where the time goes:
time: 415 us; the launch traced here: 413 us
  local copies, waits for them, and re-layouts  142 us (34%)
  Pallas kernels  86.5 us (21%)
  blocking collectives  83.2 us (20%)
  waiting for transfers between devices  44.3 us (11%)
  starting transfers between devices  41.5 us (10%)
  other arithmetic  10.5 us (3%)
  matrix products  4.53 us (1%)
    all_gather x2, blocking collectives, spectrum(): flat = lax.all_gather(scales[:, :, 0].reshape(-1), owners, axis=0)  81.1 us
    pallas_call x2, Pallas kernels, column_call(): pl.pallas_call(column_kernel, grid=(outer,), in_specs=[whole(codes.shape)...  46.7 us
    all_to_all x2, waiting for transfers between devices, spectrum(): lax.all_to_all(sorted_codes.reshape(outer, slots, sub_rows), owners, 0, 0...  44.3 us
    pallas_call x2, Pallas kernels, row_call(): pl.pallas_call(functools.partial(row_kernel, kept), grid=(kept,), in_spec...  39.8 us
    gather x2, local copies, waits for them, and re-layouts, spectrum(): table.at[place].get(mode='promise_in_bounds', unique_indices=False)  36.2 us
    unnamed x20, local copies, waits for them, and re-layouts  31.3 us
    all_to_all x2, local copies, waits for them, and re-layouts, on_device(): rows = lax.all_to_all(maps, 'phi', split_axis=1, concat_axis=2, tiled=True)  30.9 us
    all_to_all x2, starting transfers between devices, spectrum(): lax.all_to_all(sorted_codes.reshape(outer, slots, sub_rows), owners, 0, 0...  27.4 us
  transfers between devices with their start and end apart: 4, of which 1 were waited for; matrix products, arithmetic and copies ran while one was open for 31% of the time, Pallas kernels for 15%

commit v1 on v0

v1 whole, which is shorter than its diff:
```python
import functools
import math

import jax
import jax.numpy as jnp
import numpy as np
from jax import lax
from jax.experimental import pallas as pl
from jax.experimental.pallas import tpu as pltpu
from jax.sharding import PartitionSpec as P


def exact_einsum(form, table, operand):
    return jnp.einsum(form, table, operand, precision=lax.Precision.HIGHEST)


def angle_tables(row_count, start, count, modulus):
    freq_rows = jnp.arange(row_count, dtype=jnp.int32)
    sample_cols = start + jnp.arange(count, dtype=jnp.int32)
    angles = (
        2.0
        * math.pi
        / modulus
        * jnp.mod(freq_rows[:, None] * sample_cols[None, :], modulus).astype(jnp.float32)
    )
    return (jnp.cos(angles), jnp.sin(angles))


def row_transform(real_part, imag_part, outer_len, inner_len):
    row_count = real_part.shape[0]
    length = outer_len * inner_len
    cos_a, sin_a = angle_tables(outer_len, 0, outer_len, outer_len)
    real_blocks = real_part.reshape(row_count, outer_len, inner_len)
    section_real = exact_einsum("ka,rab->rkb", cos_a, real_blocks)
    section_imag = -exact_einsum("ka,rab->rkb", sin_a, real_blocks)
    if imag_part is not None:
        imag_blocks = imag_part.reshape(row_count, outer_len, inner_len)
        section_real = section_real + exact_einsum("ka,rab->rkb", sin_a, imag_blocks)
        section_imag = section_imag + exact_einsum("ka,rab->rkb", cos_a, imag_blocks)
    cos_t, sin_t = angle_tables(outer_len, 0, inner_len, length)
    turned_real = section_real * cos_t + section_imag * sin_t
    turned_imag = section_imag * cos_t - section_real * sin_t
    cos_b, sin_b = angle_tables(inner_len, 0, inner_len, inner_len)
    out_real = exact_einsum("qb,rkb->rqk", cos_b, turned_real) + exact_einsum(
        "qb,rkb->rqk", sin_b, turned_imag
    )
    out_imag = exact_einsum("qb,rkb->rqk", cos_b, turned_imag) - exact_einsum(
        "qb,rkb->rqk", sin_b, turned_real
    )
    return (out_real.reshape(row_count, length), out_imag.reshape(row_count, length))


def column_transform(real_part, imag_part, outer_len, inner_len, start):
    fields = real_part.shape[0]
    count = real_part.shape[2]
    slots = real_part.shape[3]
    length = outer_len * inner_len
    cos_a, sin_a = angle_tables(outer_len, 0, outer_len, outer_len)
    section_real = exact_einsum("ka,fabm->fkbm", cos_a, real_part) + exact_einsum(
        "ka,fabm->fkbm", sin_a, imag_part
    )
    section_imag = exact_einsum("ka,fabm->fkbm", cos_a, imag_part) - exact_einsum(
        "ka,fabm->fkbm", sin_a, real_part
    )
    cos_t, sin_t = angle_tables(outer_len, start, count, length)
    cos_t = cos_t[:, :, None]
    sin_t = sin_t[:, :, None]
    turned_real = section_real * cos_t + section_imag * sin_t
    turned_imag = section_imag * cos_t - section_real * sin_t
    cos_b, sin_b = angle_tables(inner_len, start, count, inner_len)
    out_real = exact_einsum("qb,fkbm->fqkm", cos_b, turned_real) + exact_einsum(
        "qb,fkbm->fqkm", sin_b, turned_imag
    )
    out_imag = exact_einsum("qb,fkbm->fqkm", cos_b, turned_imag) - exact_einsum(
        "qb,fkbm->fqkm", sin_b, turned_real
    )
    return (out_real.reshape(fields, length, slots), out_imag.reshape(fields, length, slots))


def accumulate(spectrum_block, table_block, spin_block, length, ell_index):
    count = table_block.shape[0]
    positions = jnp.arange(count, dtype=jnp.int32)
    freq = jnp.where(positions < length // 2, positions, positions - length)
    terms = []
    for degree in range(table_block.shape[1]):
        keep_rows = (jnp.abs(freq) <= ell_index[degree]).astype(jnp.float32)
        row_weights = spin_block[:, :, degree].astype(jnp.float32).T * keep_rows[None, :]
        table = table_block[:, degree, :].astype(jnp.float32)
        terms.append(
            jnp.einsum(
                "fk,ks,xfks->fxs",
                row_weights,
                table,
                spectrum_block,
                precision=lax.Precision.HIGHEST,
            )
        )
    return jnp.stack(terms)


def on_device_general(maps, deltas, spin_rows, ell_index, owner_map, prior):
    theta_count = lax.axis_size("theta")
    phi_count = lax.axis_size("phi")
    length = maps.shape[2] * phi_count
    values = maps.astype(jnp.float32)
    planes = jnp.stack([values[0], values[1] * values[2], values[1] * values[3]])
    row_planes = lax.all_to_all(planes, "phi", split_axis=1, concat_axis=2, tiled=True)
    inner_len = length // theta_count
    spectra = [
        row_transform(row_planes[0], None, theta_count, inner_len),
        row_transform(row_planes[1], row_planes[2], theta_count, inner_len),
    ]
    stacked = jnp.stack(
        [
            jnp.stack([spectrum[0] for spectrum in spectra]),
            jnp.stack([spectrum[1] for spectrum in spectra]),
        ]
    )
    permuted = jnp.take(stacked, owner_map, axis=3)
    columns = lax.all_to_all(permuted, "theta", split_axis=3, concat_axis=2, tiled=True)
    fields = columns.shape[1]
    slots = columns.shape[3]
    sub_rows = columns.shape[2] // theta_count
    blocks = columns.reshape(2, fields, theta_count, sub_rows, slots)
    row_start = lax.axis_index("phi") * sub_rows
    spec_real, spec_imag = column_transform(blocks[0], blocks[1], theta_count, inner_len, row_start)
    combined = jnp.stack([spec_real, spec_imag])
    totals = accumulate(
        combined,
        lax.all_gather(deltas, "phi", axis=0, tiled=True),
        lax.all_gather(spin_rows, "phi", axis=0, tiled=True),
        length,
        ell_index,
    )
    shares = lax.psum_scatter(totals, "phi", scatter_dimension=3, tiled=True)
    share_count = shares.shape[3]
    slot_start = lax.axis_index("theta") * slots + lax.axis_index("phi") * share_count
    share_ids = lax.dynamic_slice_in_dim(owner_map, slot_start, share_count)
    slot_freq = jnp.where(share_ids < length // 2, share_ids, share_ids - length)
    ell_float = ell_index.astype(jnp.float32)
    weight = 2.0 * math.pi / length * jnp.sqrt((2.0 * ell_float + 1.0) / (4.0 * math.pi)) / length
    keep_slots = (jnp.abs(slot_freq)[None, :] <= ell_index[:, None]).astype(jnp.float32) * weight[
        :, None
    ]
    scalar_real = shares[:, 0, 0] * keep_slots
    scalar_imag = shares[:, 0, 1] * keep_slots
    spin_real = shares[:, 1, 0] * keep_slots
    spin_imag = shares[:, 1, 1] * keep_slots
    coupling = (prior * jnp.sqrt(ell_float * (ell_float + 1.0)) / (length // 2))[:, None]
    inner_real = -spin_imag - coupling * scalar_real
    inner_imag = spin_real - coupling * scalar_imag
    turns = jnp.mod(-slot_freq, 4)
    phase_real = jnp.where(turns == 0, 1.0, jnp.where(turns == 2, -1.0, 0.0)).astype(jnp.float32)[
        None, :
    ]
    phase_imag = jnp.where(turns == 1, 1.0, jnp.where(turns == 3, -1.0, 0.0)).astype(jnp.float32)[
        None, :
    ]
    out_real = phase_real * inner_real - phase_imag * inner_imag
    out_imag = phase_real * inner_imag + phase_imag * inner_real
    return jnp.stack([out_real, out_imag], axis=1)


ROW_OUTER = 8
LANES = 128
VMEM_LIMIT = 67043328
CODE_TOP = 32767.0
MESH = pl.DeviceIdType.MESH


def cplx_add(x, y):
    return tuple(b if a is None else a if b is None else a + b for a, b in zip(x, y))


def cplx_sub(x, y):
    return tuple(
        (None if b is None else -b) if a is None else a if b is None else a - b
        for a, b in zip(x, y)
    )


def turn(x, step, count):
    real, imag = x
    if step == 0:
        return x
    if 4 * step == count:
        return (imag, None if real is None else -real)
    cos_v = math.cos(2.0 * math.pi * step / count)
    sin_v = math.sin(2.0 * math.pi * step / count)
    if imag is None:
        return (real * cos_v, real * -sin_v)
    if 8 * step == count:
        return ((real + imag) * cos_v, (imag - real) * cos_v)
    if 8 * step == 3 * count:
        return ((imag - real) * sin_v, (real + imag) * -sin_v)
    return (real * cos_v + imag * sin_v, imag * cos_v - real * sin_v)


def butterfly(items):
    count = len(items)
    if count == 1:
        return items
    even, odd = butterfly(items[::2]), butterfly(items[1::2])
    turned = [turn(x, step, count) for step, x in enumerate(odd)]
    return [cplx_add(a, b) for a, b in zip(even, turned)] + [
        cplx_sub(a, b) for a, b in zip(even, turned)
    ]


def split_store(high, low, where, value):
    top = value.astype(jnp.bfloat16)
    high[where] = top
    low[where] = (value - top.astype(jnp.float32)).astype(jnp.bfloat16)


def store_matrix(cos_ref, sin_ref, high, low):
    size = cos_ref.shape[0]
    first, second = slice(0, size), slice(size, 2 * size)
    cos_v, sin_v = cos_ref[...], sin_ref[...]
    split_store(high, low, (first, first), cos_v)
    split_store(high, low, (first, second), sin_v)
    split_store(high, low, (second, first), -sin_v)
    split_store(high, low, (second, second), cos_v)


def dot_nt(left, right):
    return lax.dot_general(
        left, right, (((1,), (1,)), ((), ())), preferred_element_type=jnp.float32
    )


def three_dots(mat_high, mat_low, high, low):
    return dot_nt(mat_high[...], high) + dot_nt(mat_high[...], low) + dot_nt(mat_low[...], high)


def turned(item, cos_v, sin_v):
    real, imag = item
    if imag is None:
        return real * cos_v, real * -sin_v
    return real * cos_v + imag * sin_v, imag * cos_v - real * sin_v


def flip_bits(value, mask, count):
    result, bit = 0, 1
    while bit < count:
        result = result + ((value // bit + mask // bit) % 2) * bit
        bit *= 2
    return result


def pipeline_kernel(
    peers, maps, deltas, spins, places, mirror, order, row_cos, row_sin, row_tc, row_ts,
    col_cos, col_sin, col_tc, col_ts, out_ref, land,
    planes, x_high, x_low, row_mat_high, row_mat_low, col_mat_high, col_mat_low, codes, scales,
    stage, scale_stage, recv, scale_recv, table, raw, spin_land, weights, scale_rows, scale_cols,
    total, plane_send, plane_recv, plane_own, land_send, land_recv, spin_send, spin_recv,
    raw_sem, code_send, code_recv, scale_send, scale_sem, own_sem,
):
    theta, phi = lax.axis_index("theta"), lax.axis_index("phi")
    me = theta * 2 + phi
    other = 1 - phi
    rows = planes.shape[2]
    half = planes.shape[3]
    inner = row_cos.shape[0]
    sub = col_cos.shape[0]
    groups = recv.shape[2]
    degrees = deltas.shape[1]
    slots = groups * LANES
    fold = peers // ROW_OUTER
    parts_per_half = half // inner

    def device(index):
        return {"theta": index // 2, "phi": index % 2}

    barrier = pltpu.get_barrier_semaphore()
    for mask in range(1, peers):
        pl.semaphore_signal(
            barrier, inc=1, device_id=device(flip_bits(me, mask, peers)), device_id_type=MESH
        )
    pl.semaphore_wait(barrier, peers - 1)

    def plane_copy(place):
        return pltpu.make_async_remote_copy(
            src_ref=maps.at[place, pl.ds(pl.multiple_of(other * rows, rows), rows), :],
            dst_ref=planes.at[place, 1],
            send_sem=plane_send.at[place],
            recv_sem=plane_recv.at[place],
            device_id={"phi": other},
            device_id_type=MESH,
        )

    def own_plane(place):
        return pltpu.make_async_copy(
            maps.at[place, pl.ds(pl.multiple_of(phi * rows, rows), rows), :],
            planes.at[place, 0],
            plane_own.at[place],
        )

    for place in range(4):
        plane_copy(place).start()
        own_plane(place).start()
    land_copy = pltpu.make_async_remote_copy(
        src_ref=deltas.at[:, :, pl.ds(pl.multiple_of(other * slots, slots), slots)],
        dst_ref=land,
        send_sem=land_send,
        recv_sem=land_recv,
        device_id={"phi": other},
        device_id_type=MESH,
    )
    land_copy.start()
    spin_copy = pltpu.make_async_remote_copy(
        src_ref=spins,
        dst_ref=spin_land,
        send_sem=spin_send,
        recv_sem=spin_recv,
        device_id={"phi": other},
        device_id_type=MESH,
    )
    spin_copy.start()
    store_matrix(row_cos, row_sin, row_mat_high, row_mat_low)

    sign = (1 - 2 * phi).astype(jnp.float32)

    def row_transform_kernel(places_in, kept):
        for place in places_in:
            own_plane(place).wait()
            plane_copy(place).wait_recv()
        step_rows = 16

        def chunk(step, carry):
            span = pl.ds(pl.multiple_of(step * step_rows, step_rows), step_rows)
            for first in range(0, inner, LANES):

                def part(place, a):
                    start = (a % parts_per_half) * inner + first
                    return planes[
                        place, a // parts_per_half, span, start : start + LANES
                    ].astype(jnp.float32)

                items = []
                for a in range(ROW_OUTER):
                    if len(places_in) == 1:
                        items.append((part(places_in[0], a), None))
                    else:
                        base = part(places_in[0], a)
                        items.append((base * part(places_in[1], a), base * part(places_in[2], a)))
                done = butterfly(items)
                for k in range(kept):
                    cos_k = row_tc[k : k + 1, first : first + LANES]
                    sin_k = row_ts[k : k + 1, first : first + LANES]
                    if k % 2:
                        cos_k, sin_k = cos_k * sign, sin_k * sign
                    real, imag = turned(done[k], cos_k, sin_k)
                    split_store(x_high, x_low, (k, span, slice(first, first + LANES)), real)
                    split_store(
                        x_high, x_low, (k, span, slice(inner + first, inner + first + LANES)), imag
                    )
            return carry

        lax.fori_loop(0, rows // step_rows, chunk, 0)

        def block(k, carry):
            both = three_dots(row_mat_high, row_mat_low, x_high[k], x_low[k])
            real, imag = both[:inner], both[inner:]
            top = jnp.max(jnp.maximum(jnp.abs(real), jnp.abs(imag)), axis=1, keepdims=True)
            top = jnp.maximum(top, 1e-30)
            factor = CODE_TOP / top
            code_real = jnp.round(real * factor).astype(jnp.int32)
            code_imag = jnp.round(imag * factor).astype(jnp.int32)
            span = pl.ds(pl.multiple_of(k * inner, inner), inner)
            codes[span, :] = (code_real << 16) | (code_imag & 0xFFFF)
            scales[span, :] = jnp.broadcast_to(top * (1.0 / CODE_TOP), (inner, LANES))
            return carry

        lax.fori_loop(0, kept, block, 0)

    def code_copy(field, step, source):
        group, n = step // peers, step % peers
        dest = flip_bits(me, peers - 1 - n, peers)
        return pltpu.make_async_remote_copy(
            src_ref=stage.at[field, dest, group],
            dst_ref=recv.at[field, source, group],
            send_sem=code_send.at[field, step],
            recv_sem=code_recv.at[field, source, group],
            device_id=device(dest),
            device_id_type=MESH,
        )

    def scale_copy(field, step, source):
        group, n = step // peers, step % peers
        dest = flip_bits(me, peers - 1 - n, peers)
        return pltpu.make_async_remote_copy(
            src_ref=scale_stage.at[field, dest, group],
            dst_ref=scale_recv.at[field, group, source],
            send_sem=scale_send.at[field, step],
            recv_sem=scale_sem.at[field, source, group],
            device_id=device(dest),
            device_id_type=MESH,
        )

    def own_copy(field, group):
        return pltpu.make_async_copy(
            stage.at[field, me, group], recv.at[field, me, group], own_sem.at[field, group]
        )

    lane = lax.broadcasted_iota(jnp.int32, (1, LANES), 1)
    unroll = 8

    def send_step(field, step):
        @pl.when(step % peers != peers - 1)
        def _():
            code_copy(field, step, me).start()
            scale_copy(field, step, me).start()

        @pl.when(step % peers == peers - 1)
        def _():
            own_copy(field, step // peers).start()

    def gather_and_send(field):
        def step_body(step, carry):
            group, n = step // peers, step % peers
            dest = flip_bits(me, peers - 1 - n, peers)
            first = field * peers * slots + dest * slots + group * LANES

            def rows_body(g, acc):
                base = pl.multiple_of(g * unroll, unroll)
                for u in range(unroll):
                    where = places[first + base + u]
                    stage[field, dest, group, pl.ds(base + u, 1), :] = codes[pl.ds(where, 1), :]
                    acc = jnp.where(lane == base + u, scales[pl.ds(where, 1), :], acc)
                return acc

            acc = lax.fori_loop(0, LANES // unroll, rows_body, jnp.zeros((1, LANES), jnp.float32))
            scale_stage[field, dest, group] = acc

            @pl.when(step > 0)
            def _():
                send_step(field, step - 1)

            return carry

        lax.fori_loop(0, groups * peers, step_body, 0)
        send_step(field, groups * peers - 1)

    row_transform_kernel((0,), ROW_OUTER // 2 + 1)
    gather_and_send(0)
    row_transform_kernel((1, 2, 3), ROW_OUTER)
    gather_and_send(1)

    store_matrix(col_cos, col_sin, col_mat_high, col_mat_low)
    spin_copy.wait_recv()
    eye_row = lax.broadcasted_iota(jnp.int32, (LANES, LANES), 0)
    eye_col = lax.broadcasted_iota(jnp.int32, (LANES, LANES), 1)
    eye = (eye_row == eye_col).astype(jnp.float32).astype(jnp.bfloat16)
    for which, ref in ((phi, spins), (other, spin_land)):
        for first in range(0, half, LANES):
            span = pl.ds(pl.multiple_of(which * half + first, LANES), LANES)
            weights[span, :] = dot_nt(eye, ref[:, first : first + LANES])

    raw_rows = raw.shape[1]
    raw_q = raw_rows // peers
    raw_steps = half // raw_rows

    def raw_copy(ref, lanes, step):
        return pltpu.make_async_copy(
            ref.at[pl.ds(pl.multiple_of(step * raw_rows, raw_rows), raw_rows), :, lanes],
            raw.at[step % 2],
            raw_sem.at[step % 2],
        )

    def reorder(ref, lanes, which):
        raw_copy(ref, lanes, 0).start()

        def body(step, carry):
            @pl.when(step + 1 < raw_steps)
            def _():
                raw_copy(ref, lanes, step + 1).start()

            raw_copy(ref, lanes, step).wait()
            base = pl.multiple_of(which * (sub // 2) + step * raw_q, raw_q)
            for group in range(groups):
                pieces = []
                for top in range(0, raw_rows, raw_rows // 2):
                    source = raw[
                        step % 2, top : top + raw_rows // 2, :, group * LANES : (group + 1) * LANES
                    ].reshape(raw_rows // 2 * degrees, LANES)
                    pieces.append(
                        jnp.dot(order[...], source, preferred_element_type=jnp.float32)
                    )
                small = raw_q // 2
                for k in range(peers):
                    for j in range(degrees):
                        start = (k * degrees + j) * small
                        table[group, k, j, pl.ds(base, raw_q), :] = jnp.concatenate(
                            [piece[start : start + small] for piece in pieces], axis=0
                        ).astype(jnp.bfloat16)
            return carry

        lax.fori_loop(0, raw_steps, body, 0)

    reorder(deltas, pl.ds(pl.multiple_of(phi * slots, slots), slots), phi)
    land_copy.wait_recv()
    reorder(land, pl.ds(0, slots), other)

    scale_rows[...] = jnp.zeros_like(scale_rows)

    def column_block(position, carry):
        field, group = position // groups, position % groups

        def wait_one(n, inner_carry):
            source = flip_bits(me, peers - 1 - n, peers)
            code_copy(field, group * peers + n, source).wait_recv()
            scale_copy(field, group * peers + n, source).wait_recv()
            return inner_carry

        lax.fori_loop(0, peers - 1, wait_one, 0)
        own_copy(field, group).wait()
        scale_recv[field, group, me] = scale_stage[field, me, group]

        for a in range(peers):
            scale_rows[a : a + 1, :] = scale_recv[field, group, a]
        plain = scale_rows[...]
        flips = jnp.where(field == 0, mirror[pl.ds(me * groups + group, 1), :], 1.0)
        scale_cols[0] = plain.T
        scale_cols[1] = (plain * flips).T
        step_rows = 16

        def chunk(step, inner_carry):
            span = pl.ds(pl.multiple_of(step * step_rows, step_rows), step_rows)
            sre, sim = scale_cols[0, span, :], scale_cols[1, span, :]
            for first in range(0, sub, LANES):
                items = []
                for a in range(peers):
                    code = recv[field, a, group, span, first : first + LANES]
                    real = (code >> 16).astype(jnp.float32) * sre[:, a : a + 1]
                    imag = ((code << 16) >> 16).astype(jnp.float32) * sim[:, a : a + 1]
                    items.append((real, imag))
                for k, item in enumerate(butterfly(items)):
                    real, imag = turned(
                        item,
                        col_tc[k : k + 1, first : first + LANES],
                        col_ts[k : k + 1, first : first + LANES],
                    )
                    start = (k % fold) * 2 * sub + first
                    split_store(
                        x_high, x_low, (k // fold, span, slice(start, start + LANES)), real
                    )
                    start = start + sub
                    split_store(
                        x_high, x_low, (k // fold, span, slice(start, start + LANES)), imag
                    )
            return inner_carry

        lax.fori_loop(0, LANES // step_rows, chunk, 0)
        total[...] = jnp.zeros_like(total)

        def block(k2, inner_carry):
            for r in range(fold):
                k = k2 * fold + r
                where = (k2, slice(0, LANES), slice(r * 2 * sub, (r + 1) * 2 * sub))
                both = three_dots(col_mat_high, col_mat_low, x_high[where], x_low[where])
                real, imag = both[:sub], both[sub:]
                eight = weights[pl.ds(k, sub, peers), :]
                four = jnp.where(field == 0, eight[:, :degrees], eight[:, degrees : 2 * degrees])
                for j in range(degrees):
                    weighted = table[group, k, j].astype(jnp.float32) * four[:, j : j + 1]
                    for part, value in enumerate((real, imag)):
                        total[2 * j + part] += jnp.sum(
                            (weighted * value).reshape(sub // 8, 8, LANES), axis=0
                        )
            return inner_carry

        lax.fori_loop(0, ROW_OUTER, block, 0)
        out_ref[field, group] = jnp.sum(total[...], axis=1)
        return carry

    lax.fori_loop(0, 2 * groups, column_block, 0)

    for place in range(4):
        plane_copy(place).wait_send()
    land_copy.wait_send()
    spin_copy.wait_send()

    def finish(n, carry):
        for field in range(2):
            for group in range(groups):
                code_copy(field, group * peers + n, me).wait_send()
                scale_copy(field, group * peers + n, me).wait_send()
        return carry

    lax.fori_loop(0, peers - 1, finish, 0)


def wave_tables(row_ids, col_ids, modulus):
    angles = 2.0 * math.pi / modulus * ((row_ids[:, None] * col_ids[None, :]) % modulus)
    return np.cos(angles).astype(np.float32), np.sin(angles).astype(np.float32)


def signed(ids, length):
    return jnp.where(ids < length // 2, ids, ids - length)


def pipeline_call(peers, maps, deltas, spins, places, mirror):
    fields_in, rows_all, half = maps.shape
    rows = rows_all // 2
    length = 2 * half
    slots = deltas.shape[2] // 2
    degrees = deltas.shape[1]
    groups = slots // LANES
    inner = length // ROW_OUTER
    sub = length // peers
    ids = np.arange(length)
    row_cos, row_sin = wave_tables(ids[:inner], ids[:inner], inner)
    row_tc, row_ts = wave_tables(ids[:ROW_OUTER], ids[:inner], length)
    col_cos, col_sin = wave_tables(ids[:sub], ids[:sub], sub)
    col_tc, col_ts = wave_tables(ids[:peers], ids[:sub], length)
    small = 8
    raw_rows = 2 * small * peers
    target = np.arange(small * peers * degrees)
    k, j, q = target // (degrees * small), target // small % degrees, target % small
    source = (q * peers + k) * degrees + j
    order = jnp.asarray(source[:, None] == target[None, :]).astype(jnp.bfloat16)
    bf, f32 = jnp.bfloat16, jnp.float32
    vmem = pl.BlockSpec(memory_space=pltpu.VMEM)
    anywhere = pl.BlockSpec(memory_space=pl.ANY)
    dma = pltpu.SemaphoreType.DMA
    return pl.pallas_call(
        functools.partial(pipeline_kernel, peers),
        in_specs=[anywhere, anywhere, vmem, pl.BlockSpec(memory_space=pltpu.SMEM)] + [vmem] * 10,
        out_specs=[vmem, anywhere],
        out_shape=[
            jax.ShapeDtypeStruct((2, groups, 2 * degrees, LANES), f32),
            jax.ShapeDtypeStruct((half, degrees, slots), bf),
        ],
        scratch_shapes=[
            pltpu.VMEM((fields_in, 2, rows, half), bf),
            pltpu.VMEM((ROW_OUTER, rows, 2 * inner), bf),
            pltpu.VMEM((ROW_OUTER, rows, 2 * inner), bf),
            pltpu.VMEM((2 * inner, 2 * inner), bf),
            pltpu.VMEM((2 * inner, 2 * inner), bf),
            pltpu.VMEM((2 * sub, 2 * sub), bf),
            pltpu.VMEM((2 * sub, 2 * sub), bf),
            pltpu.VMEM((length, rows), jnp.int32),
            pltpu.VMEM((length, LANES), f32),
            pltpu.VMEM((2, peers, groups, LANES, rows), jnp.int32),
            pltpu.VMEM((2, peers, groups, 1, LANES), f32),
            pltpu.VMEM((2, peers, groups, LANES, rows), jnp.int32),
            pltpu.VMEM((2, groups, peers, 1, LANES), f32),
            pltpu.VMEM((groups, peers, degrees, sub, LANES), bf),
            pltpu.VMEM((2, raw_rows, degrees, slots), bf),
            pltpu.VMEM(spins.shape, bf),
            pltpu.VMEM((length, 2 * degrees), f32),
            pltpu.VMEM((LANES, LANES), f32),
            pltpu.VMEM((2, LANES, LANES), f32),
            pltpu.VMEM((2 * degrees, 8, LANES), f32),
            dma((fields_in,)),
            dma((fields_in,)),
            dma((fields_in,)),
            dma,
            dma,
            dma,
            dma,
            dma((2,)),
            dma((2, groups * peers)),
            dma((2, peers, groups)),
            dma((2, groups * peers)),
            dma((2, peers, groups)),
            dma((2, groups)),
        ],
        compiler_params=pltpu.CompilerParams(
            vmem_limit_bytes=VMEM_LIMIT, collective_id=0, has_side_effects=True
        ),
    )(
        maps, deltas, spins, places, mirror, order, row_cos, row_sin, row_tc, row_ts,
        col_cos, col_sin, col_tc, col_ts,
    )


def on_device(maps, deltas, spin_rows, ell_index, owner_map, prior):
    phi_count = lax.axis_size("phi")
    length = maps.shape[2] * phi_count
    peers = lax.axis_size("theta") * phi_count
    half = maps.shape[2]
    degrees = deltas.shape[1]
    slots = length // peers
    inner = length // ROW_OUTER

    residue = owner_map % ROW_OUTER
    flipped = residue > ROW_OUTER // 2
    half_map = jnp.where(flipped, length - owner_map, owner_map)
    place = lambda freq: (freq % ROW_OUTER) * inner + freq // ROW_OUTER
    places = jnp.concatenate([place(half_map), place(owner_map)])
    mirror = jnp.where(flipped, -1.0, 1.0).reshape(-1, LANES)

    k_ids = lax.axis_index("phi") * half + jnp.arange(half, dtype=jnp.int32)
    keep_rows = jnp.abs(signed(k_ids, length))[None, :] <= ell_index[:, None]
    spins = jnp.where(keep_rows[None], spin_rows.transpose(1, 2, 0), 0).reshape(2 * degrees, half)
    sums, _ = pipeline_call(peers, maps, deltas, spins, places, mirror)
    sums = sums.transpose(0, 2, 1, 3).reshape(2, degrees, 2, slots)
    scalar, spin = sums[0], sums[1]

    slot_start = (lax.axis_index("theta") * phi_count + lax.axis_index("phi")) * slots
    own_ids = lax.dynamic_slice_in_dim(owner_map, slot_start, slots)
    slot_freq = signed(own_ids, length)
    ell_float = ell_index.astype(jnp.float32)
    weight = 2.0 * math.pi / length * jnp.sqrt((2.0 * ell_float + 1.0) / (4.0 * math.pi)) / length
    keep = jnp.abs(slot_freq)[None, :] <= ell_index[:, None]
    keep_slots = keep.astype(jnp.float32) * weight[:, None]
    coupling = (prior * jnp.sqrt(ell_float * (ell_float + 1.0)) / (length // 2))[:, None]
    inner_real = (-spin[:, 1] - coupling * scalar[:, 0]) * keep_slots
    inner_imag = (spin[:, 0] - coupling * scalar[:, 1]) * keep_slots
    turns = jnp.mod(-slot_freq, 4)[None, :]
    phase_real = jnp.where(turns == 0, 1.0, jnp.where(turns == 2, -1.0, 0.0))
    phase_imag = jnp.where(turns == 1, 1.0, jnp.where(turns == 3, -1.0, 0.0))
    out_real = phase_real * inner_real - phase_imag * inner_imag
    out_imag = phase_real * inner_imag + phase_imag * inner_real
    return jnp.stack([out_real, out_imag], axis=1)


def solution(mesh):
    owner_count = mesh.shape["theta"] * mesh.shape["phi"]
    paired = mesh.shape["phi"] == 2 and owner_count in (8, 16)
    body = on_device if paired else on_device_general
    placed = (
        P("grp", "theta", "phi"),
        P("phi", None, "theta"),
        P("phi", None, None),
        P(),
        P(),
        P(),
    )
    return jax.shard_map(
        body,
        mesh=mesh,
        in_specs=placed,
        out_specs=P("grp", None, ("theta", "phi")),
        check_vma=False,
    )
```

time: 415 us -> 239 us (0.58)
  Pallas kernels: 86.5 us -> 227 us
  local copies, waits for them, and re-layouts: 142 us -> 2.01 us
  blocking collectives: 83.2 us -> 0 us
  waiting for transfers between devices: 44.3 us -> 0 us
  starting transfers between devices: 41.5 us -> 0 us
  matrix products: 4.53 us -> 0 us
    pallas_call x4 -> x1, Pallas kernels: 86.5 us -> 227 us  [pipeline_call(): pl.pallas_call(functools.partial(pipeline_kernel, peers), in_specs=[anywh...]
    all_gather x3 -> x0, blocking collectives: 83.2 us -> none  [the longest x2 81.1 us: spectrum(): flat = lax.all_gather(scales[:, :, 0].reshape(-1), owners, axis=0)]
    all_to_all x4 -> x0, local copies, waits for them, and re-layouts: 53.6 us -> none  [the longest x2 30.9 us: on_device(): rows = lax.all_to_all(maps, 'phi', split_axis=1, concat_axis=2, tiled=True)]
    all_to_all x4 -> x0, waiting for transfers between devices: 44.3 us -> none  [the longest x2 44.3 us: spectrum(): lax.all_to_all(sorted_codes.reshape(outer, slots, sub_rows), owners, 0, 0...]
    all_to_all x4 -> x0, starting transfers between devices: 41.5 us -> none  [the longest x2 27.4 us: spectrum(): lax.all_to_all(sorted_codes.reshape(outer, slots, sub_rows), owners, 0, 0...]
    gather x2 -> x0, local copies, waits for them, and re-layouts: 36.2 us -> none  [spectrum(): table.at[place].get(mode='promise_in_bounds', unique_indices=False)]
    unnamed x20 -> x0, local copies, waits for them, and re-layouts: 31.3 us -> none
    reshape x5 -> x1, local copies, waits for them, and re-layouts: 16.5 us -> 0.63 us  [on_device(): jnp.where(keep_rows[None], spin_rows.transpose(1, 2, 0), 0)]
  transfers between devices with their start and end apart: 4 -> 0, of which waited for: 1 -> 0; matrix products, arithmetic and copies ran while one was open for 31% -> 0% of each run, Pallas kernels for 15% -> 0%
where the time goes in v1:
time: 239 us
  Pallas kernels  227 us (95%)
  other arithmetic  9.65 us (4%)
    pallas_call x1, Pallas kernels, pipeline_call(): pl.pallas_call(functools.partial(pipeline_kernel, peers), in_specs=[anywh...  227 us

profile of v1, /device:TPU:0, one launch (start us, length us, event | category | flops | bytes accessed | tf_op | source)
XLA Modules:
  0.0 238.7 jit_solution(5340552073136459712)
XLA Ops:
  0.0 1.3 compare_select_fusion.7
  1.3 0.6 compare_select_fusion.5
  1.9 1.3 fusion.17
  3.3 0.8 fusion.1
  4.0 0.6 pad_add_fusion.places
  4.6 0.7 broadcast_compare_fusion
  5.4 0.8 bitcast_select_fusion
  6.2 0.6 reshape.161.spins
  6.8 1.3 select_bitcast_fusion.mirror
  8.1 227.0 %shard_map.145 = (f32[2,2,8,128]{3,2,1,0:T(8,128)}, bf16[2048,4,256]{2,1,0:T(4,128)(2,1)}) custom-call(bf16[4,512,2048]{2,1,0:T(8,128)(2,1)} %maps.1, bf16[2048,4,512]{2,1,0:T(4,128)(2,1)} %deltas.1, bf16[8,2048]{1,0:T(8,128)(2,1)} %reshape.161.spins, s32[8192]{0:T(1024)} %pad_add_fusion.places, f32[32,128]{1,0:T(8,128)} %select_bitcast_fusion.mirror, ...), custom_call_target="tpu_custom_call" | custom-call | tf_op jit(solution)/shard_map/pallas_call | solution.py:627
  235.1 0.7 fusion.18
  235.9 0.7 fusion.16
  236.6 0.8 multiply_subtract_fusion
  237.4 0.7 multiply_add_fusion
  238.1 0.6 copy.24
  (7 shorter events, 0.1 us)

commit v2 on v1

--- a/solution.py
+++ b/solution.py
@@ -213,10 +213,9 @@
     low[where] = (value - top.astype(jnp.float32)).astype(jnp.bfloat16)
 
 
-def store_matrix(cos_ref, sin_ref, high, low):
-    size = cos_ref.shape[0]
+def store_matrix(cos_v, sin_v, high, low):
+    size = cos_v.shape[0]
     first, second = slice(0, size), slice(size, 2 * size)
-    cos_v, sin_v = cos_ref[...], sin_ref[...]
     split_store(high, low, (first, first), cos_v)
     split_store(high, low, (first, second), sin_v)
     split_store(high, low, (second, first), -sin_v)
@@ -249,24 +248,28 @@
 
 
 def pipeline_kernel(
-    peers, maps, deltas, spins, places, mirror, order, row_cos, row_sin, row_tc, row_ts,
-    col_cos, col_sin, col_tc, col_ts, out_ref, land,
-    planes, x_high, x_low, row_mat_high, row_mat_low, col_mat_high, col_mat_low, codes, scales,
-    stage, scale_stage, recv, scale_recv, table, raw, spin_land, weights, scale_rows, scale_cols,
-    total, plane_send, plane_recv, plane_own, land_send, land_recv, spin_send, spin_recv,
-    raw_sem, code_send, code_recv, scale_send, scale_sem, own_sem,
+    peers, maps, deltas, spins, owner, owner_rows, ells, priors, row_cos, row_sin, row_tc, row_ts,
+    col_tc, col_ts, out_ref, land,
+    planes, far_plane, x_high, x_low, row_mat_high, row_mat_low, col_mat_high, col_mat_low,
+    codes, scales, stage, scale_stage, recv, scale_recv, table, raw, order, spin_land, weights,
+    scale_rows, scale_cols, total, sums, plane_send, plane_recv, plane_own, far_send, far_recv,
+    land_send, land_recv, spin_send, spin_recv, raw_sem, code_send, code_recv, scale_send,
+    scale_sem, own_sem,
 ):
     theta, phi = lax.axis_index("theta"), lax.axis_index("phi")
     me = theta * 2 + phi
     other = 1 - phi
     rows = planes.shape[2]
     half = planes.shape[3]
+    length = 2 * half
     inner = row_cos.shape[0]
-    sub = col_cos.shape[0]
+    sub = col_tc.shape[1]
     groups = recv.shape[2]
     degrees = deltas.shape[1]
     slots = groups * LANES
-    fold = peers // ROW_OUTER
+    fold = rows // LANES
+    near = peers // 2
+    far_me = flip_bits(me, near, peers)
     parts_per_half = half // inner
 
     def device(index):
@@ -278,6 +281,17 @@
             barrier, inc=1, device_id=device(flip_bits(me, mask, peers)), device_id_type=MESH
         )
     pl.semaphore_wait(barrier, peers - 1)
+
+    def far_copy(swap):
+        target = (phi + swap) % 2
+        return pltpu.make_async_remote_copy(
+            src_ref=maps.at[0, pl.ds(pl.multiple_of(target * rows, rows), rows), :],
+            dst_ref=far_plane.at[0, swap],
+            send_sem=far_send.at[swap],
+            recv_sem=far_recv.at[swap],
+            device_id=device(flip_bits(me, near + swap, peers)),
+            device_id_type=MESH,
+        )
 
     def plane_copy(place):
         return pltpu.make_async_remote_copy(
@@ -296,6 +310,8 @@
             plane_own.at[place],
         )
 
+    for swap in range(2):
+        far_copy(swap).start()
     for place in range(4):
         plane_copy(place).start()
         own_plane(place).start()
@@ -317,14 +333,11 @@
         device_id_type=MESH,
     )
     spin_copy.start()
-    store_matrix(row_cos, row_sin, row_mat_high, row_mat_low)
+    store_matrix(row_cos[...], row_sin[...], row_mat_high, row_mat_low)
 
     sign = (1 - 2 * phi).astype(jnp.float32)
 
-    def row_transform_kernel(places_in, kept):
-        for place in places_in:
-            own_plane(place).wait()
-            plane_copy(place).wait_recv()
+    def row_transform_kernel(source, places_in, kept):
         step_rows = 16
 
         def chunk(step, carry):
@@ -333,7 +346,7 @@
 
                 def part(place, a):
                     start = (a % parts_per_half) * inner + first
-                    return planes[
+                    return source[
                         place, a // parts_per_half, span, start : start + LANES
                     ].astype(jnp.float32)
 
@@ -374,92 +387,155 @@
 
         lax.fori_loop(0, kept, block, 0)
 
-    def code_copy(field, step, source):
-        group, n = step // peers, step % peers
-        dest = flip_bits(me, peers - 1 - n, peers)
+    def mask_of(count, n):
+        if count == peers:
+            return peers - 1 - n // 2 - near * (n % 2)
+        return count - 1 - n
+
+    def code_copy(field, slot, group, mask, source):
         return pltpu.make_async_remote_copy(
-            src_ref=stage.at[field, dest, group],
+            src_ref=stage.at[field, slot, group],
             dst_ref=recv.at[field, source, group],
-            send_sem=code_send.at[field, step],
+            send_sem=code_send.at[field, slot, group],
             recv_sem=code_recv.at[field, source, group],
-            device_id=device(dest),
+            device_id=device(flip_bits(me, mask, peers)),
             device_id_type=MESH,
         )
 
-    def scale_copy(field, step, source):
-        group, n = step // peers, step % peers
-        dest = flip_bits(me, peers - 1 - n, peers)
+    def scale_copy(field, slot, group, mask, source):
         return pltpu.make_async_remote_copy(
-            src_ref=scale_stage.at[field, dest, group],
+            src_ref=scale_stage.at[field, slot, group],
             dst_ref=scale_recv.at[field, group, source],
-            send_sem=scale_send.at[field, step],
+            send_sem=scale_send.at[field, slot, group],
             recv_sem=scale_sem.at[field, source, group],
-            device_id=device(dest),
+            device_id=device(flip_bits(me, mask, peers)),
             device_id_type=MESH,
         )
 
-    def own_copy(field, group):
+    def own_copy(field, slot, group, source, which):
         return pltpu.make_async_copy(
-            stage.at[field, me, group], recv.at[field, me, group], own_sem.at[field, group]
+            stage.at[field, slot, group], recv.at[field, source, group], own_sem.at[which, group]
         )
 
     lane = lax.broadcasted_iota(jnp.int32, (1, LANES), 1)
     unroll = 8
-
-    def send_step(field, step):
-        @pl.when(step % peers != peers - 1)
+    shift = ROW_OUTER.bit_length() - 1
+
+    def send_block(field, base, count, group, n, source, which):
+        @pl.when(n != count - 1)
         def _():
-            code_copy(field, step, me).start()
-            scale_copy(field, step, me).start()
-
-        @pl.when(step % peers == peers - 1)
+            mask = mask_of(count, n)
+            code_copy(field, base + n, group, mask, source).start()
+            scale_copy(field, base + n, group, mask, source).start()
+
+        @pl.when(n == count - 1)
         def _():
-            own_copy(field, step // peers).start()
-
-    def gather_and_send(field):
+            own_copy(field, base + n, group, source, which).start()
+
+    def gather_blocks(field, base, count, first_group, last_group, source, which, send):
         def step_body(step, carry):
-            group, n = step // peers, step % peers
-            dest = flip_bits(me, peers - 1 - n, peers)
-            first = field * peers * slots + dest * slots + group * LANES
+            group, n = step // count, step % count
+            dest = flip_bits(me, mask_of(count, n), peers)
+            first = dest * slots + group * LANES
 
             def rows_body(g, acc):
-                base = pl.multiple_of(g * unroll, unroll)
+                start = pl.multiple_of(g * unroll, unroll)
                 for u in range(unroll):
-                    where = places[first + base + u]
-                    stage[field, dest, group, pl.ds(base + u, 1), :] = codes[pl.ds(where, 1), :]
-                    acc = jnp.where(lane == base + u, scales[pl.ds(where, 1), :], acc)
+                    freq = owner[first + start + u]
+                    if field == 0:
+                        mirrored = (freq & (ROW_OUTER - 1)) > ROW_OUTER // 2
+                        freq = jnp.where(mirrored, length - freq, freq)
+                    where = (freq & (ROW_OUTER - 1)) * inner + (freq >> shift)
+                    stage[field, base + n, group, pl.ds(start + u, 1), :] = codes[
+                        pl.ds(where, 1), :
+                    ]
+                    acc = jnp.where(lane == start + u, scales[pl.ds(where, 1), :], acc)
                 return acc
 
             acc = lax.fori_loop(0, LANES // unroll, rows_body, jnp.zeros((1, LANES), jnp.float32))
-            scale_stage[field, dest, group] = acc
-
-            @pl.when(step > 0)
-            def _():
-                send_step(field, step - 1)
+            scale_stage[field, base + n, group] = acc
+
+            if send:
+
+                @pl.when(step > first_group * count)
+                def _():
+                    before = step - 1
+                    send_block(field, base, count, before // count, before % count, source, which)
 
             return carry
 
-        lax.fori_loop(0, groups * peers, step_body, 0)
-        send_step(field, groups * peers - 1)
-
-    row_transform_kernel((0,), ROW_OUTER // 2 + 1)
-    gather_and_send(0)
-    row_transform_kernel((1, 2, 3), ROW_OUTER)
-    gather_and_send(1)
-
-    store_matrix(col_cos, col_sin, col_mat_high, col_mat_low)
+        lax.fori_loop(first_group * count, last_group * count, step_body, 0)
+        if send:
+            send_block(field, base, count, last_group - 1, count - 1, source, which)
+
+    own_plane(0).wait()
+    plane_copy(0).wait_recv()
+    row_transform_kernel(planes, (0,), ROW_OUTER // 2 + 1)
+    gather_blocks(0, 0, near, 0, groups, me, 0, True)
+    for place in range(1, 4):
+        own_plane(place).wait()
+        plane_copy(place).wait_recv()
+    row_transform_kernel(planes, (1, 2, 3), ROW_OUTER)
+    gather_blocks(1, 0, peers, 0, groups - 1, me, 2, True)
+    gather_blocks(1, 0, peers, groups - 1, groups, me, 2, False)
+
+    for swap in range(2):
+        far_copy(swap).wait_recv()
+    row_transform_kernel(far_plane, (0,), ROW_OUTER // 2 + 1)
+    gather_blocks(0, near, near, 0, groups, far_me, 1, True)
+
+    def send_last(n, carry):
+        send_block(1, 0, peers, groups - 1, n, me, 2)
+        return carry
+
+    lax.fori_loop(0, peers, send_last, 0)
+
+    skip = inner // sub
+    thinned = []
+    for index, wave in enumerate((row_cos, row_sin)):
+        for first in range(0, sub, LANES):
+            start = index * inner * (sub // LANES) + first // LANES * inner
+            scales[start : start + inner, :] = wave[:, first : first + LANES]
+        thinned.append(
+            jnp.concatenate(
+                [
+                    scales[
+                        pl.ds(index * inner * (sub // LANES) + first // LANES * inner, sub, skip), :
+                    ]
+                    for first in range(0, sub, LANES)
+                ],
+                axis=1,
+            )
+        )
+    store_matrix(*thinned, col_mat_high, col_mat_low)
     spin_copy.wait_recv()
     eye_row = lax.broadcasted_iota(jnp.int32, (LANES, LANES), 0)
     eye_col = lax.broadcasted_iota(jnp.int32, (LANES, LANES), 1)
     eye = (eye_row == eye_col).astype(jnp.float32).astype(jnp.bfloat16)
+    column = lax.broadcasted_iota(jnp.int32, (1, degrees), 1)
+    bound = jnp.zeros((1, degrees), jnp.int32)
+    for j in range(degrees):
+        bound = jnp.where(column == j, ells[j], bound)
     for which, ref in ((phi, spins), (other, spin_land)):
         for first in range(0, half, LANES):
-            span = pl.ds(pl.multiple_of(which * half + first, LANES), LANES)
-            weights[span, :] = dot_nt(eye, ref[:, first : first + LANES])
+            start = pl.multiple_of(which * half + first, LANES)
+            span = pl.ds(start, LANES)
+            k_id = lax.broadcasted_iota(jnp.int32, (LANES, 1), 0) + start
+            keep = jnp.abs(signed(k_id, length)) <= bound
+            for spin in range(2):
+                value = dot_nt(eye, ref[spin, :, first : first + LANES])
+                weights[span, spin * degrees : (spin + 1) * degrees] = jnp.where(keep, value, 0.0)
 
     raw_rows = raw.shape[1]
     raw_q = raw_rows // peers
     raw_steps = half // raw_rows
+    small = raw_q // 2
+    width = small * peers * degrees
+    target = lax.broadcasted_iota(jnp.int32, (width, width), 0)
+    source_row = lax.broadcasted_iota(jnp.int32, (width, width), 1)
+    polar, degree_id = source_row // degrees, source_row % degrees
+    wanted = (polar % peers * degrees + degree_id) * small + polar // peers
+    order[...] = (wanted == target).astype(jnp.float32).astype(jnp.bfloat16)
 
     def raw_copy(ref, lanes, step):
         return pltpu.make_async_copy(
@@ -487,7 +563,6 @@
                     pieces.append(
                         jnp.dot(order[...], source, preferred_element_type=jnp.float32)
                     )
-                small = raw_q // 2
                 for k in range(peers):
                     for j in range(degrees):
                         start = (k * degrees + j) * small
@@ -505,24 +580,51 @@
     scale_rows[...] = jnp.zeros_like(scale_rows)
 
     def column_block(position, carry):
-        field, group = position // groups, position % groups
-
-        def wait_one(n, inner_carry):
-            source = flip_bits(me, peers - 1 - n, peers)
-            code_copy(field, group * peers + n, source).wait_recv()
-            scale_copy(field, group * peers + n, source).wait_recv()
-            return inner_carry
-
-        lax.fori_loop(0, peers - 1, wait_one, 0)
-        own_copy(field, group).wait()
-        scale_recv[field, group, me] = scale_stage[field, me, group]
+        early = position < groups - 1
+        scalar_turn = (position >= groups - 1) & (position < 2 * groups - 1)
+        field = jnp.where(scalar_turn, 0, 1)
+        group = jnp.where(
+            early, position, jnp.where(scalar_turn, position - (groups - 1), groups - 1)
+        )
+
+        @pl.when(field == 0)
+        def _():
+            def wait_one(n, inner_carry):
+                mask = mask_of(near, n)
+                peer = flip_bits(me, mask, peers)
+                code_copy(0, n, group, mask, peer).wait_recv()
+                scale_copy(0, n, group, mask, peer).wait_recv()
+                across = flip_bits(peer, near, peers)
+                code_copy(0, near + n, group, mask, across).wait_recv()
+                scale_copy(0, near + n, group, mask, across).wait_recv()
+                return inner_carry
+
+            lax.fori_loop(0, near - 1, wait_one, 0)
+            own_copy(0, near - 1, group, me, 0).wait()
+            own_copy(0, 2 * near - 1, group, far_me, 1).wait()
+            scale_recv[0, group, me] = scale_stage[0, near - 1, group]
+            scale_recv[0, group, far_me] = scale_stage[0, 2 * near - 1, group]
+
+        @pl.when(field == 1)
+        def _():
+            def wait_one(n, inner_carry):
+                mask = mask_of(peers, n)
+                peer = flip_bits(me, mask, peers)
+                code_copy(1, n, group, mask, peer).wait_recv()
+                scale_copy(1, n, group, mask, peer).wait_recv()
+                return inner_carry
+
+            lax.fori_loop(0, peers - 1, wait_one, 0)
+            own_copy(1, peers - 1, group, me, 2).wait()
+            scale_recv[1, group, me] = scale_stage[1, peers - 1, group]
 
         for a in range(peers):
             scale_rows[a : a + 1, :] = scale_recv[field, group, a]
         plain = scale_rows[...]
-        flips = jnp.where(field == 0, mirror[pl.ds(me * groups + group, 1), :], 1.0)
+        own_freq = owner_rows[pl.ds(me * groups + group, 1), :]
+        mirrored = ((own_freq & (ROW_OUTER - 1)) > ROW_OUTER // 2) & (field == 0)
         scale_cols[0] = plain.T
-        scale_cols[1] = (plain * flips).T
+        scale_cols[1] = jnp.where(mirrored, -plain, plain).T
         step_rows = 16
 
         def chunk(step, inner_carry):
@@ -541,13 +643,14 @@
                         col_tc[k : k + 1, first : first + LANES],
                         col_ts[k : k + 1, first : first + LANES],
                     )
-                    start = (k % fold) * 2 * sub + first
+                    start = pl.multiple_of(k % fold * LANES + step * step_rows, step_rows)
+                    place = pl.ds(start, step_rows)
                     split_store(
-                        x_high, x_low, (k // fold, span, slice(start, start + LANES)), real
+                        x_high, x_low, (k // fold, place, slice(first, first + LANES)), real
                     )
-                    start = start + sub
                     split_store(
-                        x_high, x_low, (k // fold, span, slice(start, start + LANES)), imag
+                        x_high, x_low,
+                        (k // fold, place, slice(sub + first, sub + first + LANES)), imag,
                     )
             return inner_carry
 
@@ -555,11 +658,12 @@
         total[...] = jnp.zeros_like(total)
 
         def block(k2, inner_carry):
+            where = (k2, slice(0, rows), slice(0, 2 * sub))
+            both = three_dots(col_mat_high, col_mat_low, x_high[where], x_low[where])
             for r in range(fold):
                 k = k2 * fold + r
-                where = (k2, slice(0, LANES), slice(r * 2 * sub, (r + 1) * 2 * sub))
-                both = three_dots(col_mat_high, col_mat_low, x_high[where], x_low[where])
-                real, imag = both[:sub], both[sub:]
+                span = slice(r * LANES, (r + 1) * LANES)
+                real, imag = both[:sub, span], both[sub:, span]
                 eight = weights[pl.ds(k, sub, peers), :]
                 four = jnp.where(field == 0, eight[:, :degrees], eight[:, degrees : 2 * degrees])
                 for j in range(degrees):
@@ -570,25 +674,52 @@
                         )
             return inner_carry
 
-        lax.fori_loop(0, ROW_OUTER, block, 0)
-        out_ref[field, group] = jnp.sum(total[...], axis=1)
+        lax.fori_loop(0, peers // fold, block, 0)
+        sums[field, group] = jnp.sum(total[...], axis=1)
         return carry
 
     lax.fori_loop(0, 2 * groups, column_block, 0)
+
+    for group in range(groups):
+        slot_freq = signed(owner_rows[pl.ds(me * groups + group, 1), :], length)
+        turns = -slot_freq & 3
+        phase_real = jnp.where(turns == 0, 1.0, jnp.where(turns == 2, -1.0, 0.0))
+        phase_imag = jnp.where(turns == 1, 1.0, jnp.where(turns == 3, -1.0, 0.0))
+        scalar, spin = sums[0, group], sums[1, group]
+        for j in range(degrees):
+            ell = jnp.full((1, LANES), ells[j], jnp.int32)
+            ell_float = ell.astype(jnp.float32)
+            weight = jnp.sqrt((2.0 * ell_float + 1.0) / (4.0 * math.pi))
+            weight = weight * (2.0 * math.pi / length / length)
+            keep = jnp.where(jnp.abs(slot_freq) <= ell, weight, 0.0)
+            coupling = priors[j] * jnp.sqrt(ell_float * (ell_float + 1.0)) * (2.0 / length)
+            re, im = 2 * j, 2 * j + 1
+            inner_real = (-spin[im : im + 1] - coupling * scalar[re : re + 1]) * keep
+            inner_imag = (spin[re : re + 1] - coupling * scalar[im : im + 1]) * keep
+            span = slice(group * LANES, (group + 1) * LANES)
+            out_ref[j, 0:1, span] = phase_real * inner_real - phase_imag * inner_imag
+            out_ref[j, 1:2, span] = phase_real * inner_imag + phase_imag * inner_real
 
     for place in range(4):
         plane_copy(place).wait_send()
+    for swap in range(2):
+        far_copy(swap).wait_send()
     land_copy.wait_send()
     spin_copy.wait_send()
 
-    def finish(n, carry):
-        for field in range(2):
+    def finish(count):
+        def body(n, carry):
             for group in range(groups):
-                code_copy(field, group * peers + n, me).wait_send()
-                scale_copy(field, group * peers + n, me).wait_send()
-        return carry
-
-    lax.fori_loop(0, peers - 1, finish, 0)
+                for field, base in ((0, 0), (0, near)) if count == near else ((1, 0),):
+                    mask = mask_of(count, n)
+                    code_copy(field, base + n, group, mask, me).wait_send()
+                    scale_copy(field, base + n, group, mask, me).wait_send()
+            return carry
+
+        lax.fori_loop(0, count - 1, body, 0)
+
+    finish(near)
+    finish(peers)
 
 
 def wave_tables(row_ids, col_ids, modulus):
@@ -600,7 +731,7 @@
     return jnp.where(ids < length // 2, ids, ids - length)
 
 
-def pipeline_call(peers, maps, deltas, spins, places, mirror):
+def pipeline_call(peers, maps, deltas, spins, owner_map, ell_index, prior):
     fields_in, rows_all, half = maps.shape
     rows = rows_all // 2
     length = 2 * half
@@ -612,28 +743,26 @@
     ids = np.arange(length)
     row_cos, row_sin = wave_tables(ids[:inner], ids[:inner], inner)
     row_tc, row_ts = wave_tables(ids[:ROW_OUTER], ids[:inner], length)
-    col_cos, col_sin = wave_tables(ids[:sub], ids[:sub], sub)
     col_tc, col_ts = wave_tables(ids[:peers], ids[:sub], length)
     small = 8
     raw_rows = 2 * small * peers
-    target = np.arange(small * peers * degrees)
-    k, j, q = target // (degrees * small), target // small % degrees, target % small
-    source = (q * peers + k) * degrees + j
-    order = jnp.asarray(source[:, None] == target[None, :]).astype(jnp.bfloat16)
+    width = small * peers * degrees
     bf, f32 = jnp.bfloat16, jnp.float32
     vmem = pl.BlockSpec(memory_space=pltpu.VMEM)
+    smem = pl.BlockSpec(memory_space=pltpu.SMEM)
     anywhere = pl.BlockSpec(memory_space=pl.ANY)
     dma = pltpu.SemaphoreType.DMA
     return pl.pallas_call(
         functools.partial(pipeline_kernel, peers),
-        in_specs=[anywhere, anywhere, vmem, pl.BlockSpec(memory_space=pltpu.SMEM)] + [vmem] * 10,
+        in_specs=[anywhere, anywhere, vmem, smem, vmem, smem, smem] + [vmem] * 6,
         out_specs=[vmem, anywhere],
         out_shape=[
-            jax.ShapeDtypeStruct((2, groups, 2 * degrees, LANES), f32),
+            jax.ShapeDtypeStruct((degrees, 2, slots), f32),
             jax.ShapeDtypeStruct((half, degrees, slots), bf),
         ],
         scratch_shapes=[
             pltpu.VMEM((fields_in, 2, rows, half), bf),
+            pltpu.VMEM((1, 2, rows, half), bf),
             pltpu.VMEM((ROW_OUTER, rows, 2 * inner), bf),
             pltpu.VMEM((ROW_OUTER, rows, 2 * inner), bf),
             pltpu.VMEM((2 * inner, 2 * inner), bf),
@@ -648,78 +777,47 @@
             pltpu.VMEM((2, groups, peers, 1, LANES), f32),
             pltpu.VMEM((groups, peers, degrees, sub, LANES), bf),
             pltpu.VMEM((2, raw_rows, degrees, slots), bf),
+            pltpu.VMEM((width, width), bf),
             pltpu.VMEM(spins.shape, bf),
             pltpu.VMEM((length, 2 * degrees), f32),
             pltpu.VMEM((LANES, LANES), f32),
             pltpu.VMEM((2, LANES, LANES), f32),
             pltpu.VMEM((2 * degrees, 8, LANES), f32),
+            pltpu.VMEM((2, groups, 2 * degrees, LANES), f32),
             dma((fields_in,)),
             dma((fields_in,)),
             dma((fields_in,)),
+            dma((2,)),
+            dma((2,)),
             dma,
             dma,
             dma,
             dma,
             dma((2,)),
-            dma((2, groups * peers)),
             dma((2, peers, groups)),
-            dma((2, groups * peers)),
             dma((2, peers, groups)),
-            dma((2, groups)),
+            dma((2, peers, groups)),
+            dma((2, peers, groups)),
+            dma((3, groups)),
         ],
         compiler_params=pltpu.CompilerParams(
             vmem_limit_bytes=VMEM_LIMIT, collective_id=0, has_side_effects=True
         ),
     )(
-        maps, deltas, spins, places, mirror, order, row_cos, row_sin, row_tc, row_ts,
-        col_cos, col_sin, col_tc, col_ts,
-    )
+        maps, deltas, spins, owner_map, owner_map.reshape(-1, LANES), ell_index, prior,
+        row_cos, row_sin, row_tc, row_ts, col_tc, col_ts,
+    )[0]
 
 
 def on_device(maps, deltas, spin_rows, ell_index, owner_map, prior):
-    phi_count = lax.axis_size("phi")
-    length = maps.shape[2] * phi_count
-    peers = lax.axis_size("theta") * phi_count
-    half = maps.shape[2]
-    degrees = deltas.shape[1]
-    slots = length // peers
-    inner = length // ROW_OUTER
-
-    residue = owner_map % ROW_OUTER
-    flipped = residue > ROW_OUTER // 2
-    half_map = jnp.where(flipped, length - owner_map, owner_map)
-    place = lambda freq: (freq % ROW_OUTER) * inner + freq // ROW_OUTER
-    places = jnp.concatenate([place(half_map), place(owner_map)])
-    mirror = jnp.where(flipped, -1.0, 1.0).reshape(-1, LANES)
-
-    k_ids = lax.axis_index("phi") * half + jnp.arange(half, dtype=jnp.int32)
-    keep_rows = jnp.abs(signed(k_ids, length))[None, :] <= ell_index[:, None]
-    spins = jnp.where(keep_rows[None], spin_rows.transpose(1, 2, 0), 0).reshape(2 * degrees, half)
-    sums, _ = pipeline_call(peers, maps, deltas, spins, places, mirror)
-    sums = sums.transpose(0, 2, 1, 3).reshape(2, degrees, 2, slots)
-    scalar, spin = sums[0], sums[1]
-
-    slot_start = (lax.axis_index("theta") * phi_count + lax.axis_index("phi")) * slots
-    own_ids = lax.dynamic_slice_in_dim(owner_map, slot_start, slots)
-    slot_freq = signed(own_ids, length)
-    ell_float = ell_index.astype(jnp.float32)
-    weight = 2.0 * math.pi / length * jnp.sqrt((2.0 * ell_float + 1.0) / (4.0 * math.pi)) / length
-    keep = jnp.abs(slot_freq)[None, :] <= ell_index[:, None]
-    keep_slots = keep.astype(jnp.float32) * weight[:, None]
-    coupling = (prior * jnp.sqrt(ell_float * (ell_float + 1.0)) / (length // 2))[:, None]
-    inner_real = (-spin[:, 1] - coupling * scalar[:, 0]) * keep_slots
-    inner_imag = (spin[:, 0] - coupling * scalar[:, 1]) * keep_slots
-    turns = jnp.mod(-slot_freq, 4)[None, :]
-    phase_real = jnp.where(turns == 0, 1.0, jnp.where(turns == 2, -1.0, 0.0))
-    phase_imag = jnp.where(turns == 1, 1.0, jnp.where(turns == 3, -1.0, 0.0))
-    out_real = phase_real * inner_real - phase_imag * inner_imag
-    out_imag = phase_real * inner_imag + phase_imag * inner_real
-    return jnp.stack([out_real, out_imag], axis=1)
+    peers = lax.axis_size("theta") * lax.axis_size("phi")
+    spins = spin_rows.transpose(1, 2, 0)
+    return pipeline_call(peers, maps, deltas, spins, owner_map, ell_index, prior)
 
 
 def solution(mesh):
     owner_count = mesh.shape["theta"] * mesh.shape["phi"]
-    paired = mesh.shape["phi"] == 2 and owner_count in (8, 16)
+    paired = mesh.shape["phi"] == 2 and owner_count == 16
     body = on_device if paired else on_device_general
     placed = (
         P("grp", "theta", "phi"),

time: 239 us -> 212 us (0.89)
  Pallas kernels: 227 us -> 210 us
  other arithmetic: 9.65 us -> 0 us
    pallas_call x1, Pallas kernels: 227 us -> 210 us  [pipeline_call(): pl.pallas_call(functools.partial(pipeline_kernel, peers), in_specs=[anywh...]
    select_n x3 -> x0, other arithmetic: 2.71 us -> none  [the longest x1 1.33 us: on_device(): phase_real = jnp.where(turns == 0, 1.0, jnp.where(turns == 2, -1.0, 0.0))]
where the time goes in v2:
time: 212 us; the launch traced here: 211 us
  Pallas kernels  210 us (99%)
    pallas_call x1, Pallas kernels, pipeline_call(): pl.pallas_call(functools.partial(pipeline_kernel, peers), in_specs=[anywh...  210 us

profile of v2, /device:TPU:0, one launch (start us, length us, event | category | flops | bytes accessed | tf_op | source)
XLA Modules:
  0.0 211.1 jit_solution(18355996317708914959)
XLA Ops:
  0.0 209.8 %shard_map.118 = (f32[4,2,256]{2,1,0:T(2,128)}, bf16[2048,4,256]{2,1,0:T(4,128)(2,1)}) custom-call(bf16[4,512,2048]{2,1,0:T(8,128)(2,1)} %maps.1, bf16[2048,4,512]{2,1,0:T(4,128)(2,1)} %deltas.1, bf16[2,4,2048]{2,1,0:T(4,128)(2,1)} %bitcast.3, s32[4096]{0:T(1024)} %owner.1, s32[32,128]{1,0:T(8,128)} %bitcast.2, s32[4]{0:T(128)} %ells.1, f32[4]{0:T(128)} %priors.1, ...), custom_call_target="tpu_custom_call" | custom-call | tf_op jit(solution)/shard_map/pallas_call | solution.py:755
  209.8 1.3 copy.14

commit v3 on v2

--- a/solution.py
+++ b/solution.py
@@ -163,6 +163,7 @@
 
 ROW_OUTER = 8
 LANES = 128
+BLOCK = 64
 VMEM_LIMIT = 67043328
 CODE_TOP = 32767.0
 MESH = pl.DeviceIdType.MESH
@@ -266,8 +267,10 @@
     sub = col_tc.shape[1]
     groups = recv.shape[2]
     degrees = deltas.shape[1]
-    slots = groups * LANES
-    fold = rows // LANES
+    slots = groups * BLOCK
+    fold = rows // BLOCK
+    early = 1
+    split = LANES // BLOCK
     near = peers // 2
     far_me = flip_bits(me, near, peers)
     parts_per_half = half // inner
@@ -432,11 +435,12 @@
         def _():
             own_copy(field, base + n, group, source, which).start()
 
-    def gather_blocks(field, base, count, first_group, last_group, source, which, send):
+    def gather_blocks(field, base, count, source, which, sent_groups):
         def step_body(step, carry):
             group, n = step // count, step % count
             dest = flip_bits(me, mask_of(count, n), peers)
-            first = dest * slots + group * LANES
+            first = dest * slots + group * BLOCK
+            shown = lane - group % split * BLOCK
 
             def rows_body(g, acc):
                 start = pl.multiple_of(g * unroll, unroll)
@@ -449,46 +453,43 @@
                     stage[field, base + n, group, pl.ds(start + u, 1), :] = codes[
                         pl.ds(where, 1), :
                     ]
-                    acc = jnp.where(lane == start + u, scales[pl.ds(where, 1), :], acc)
+                    acc = jnp.where(shown == start + u, scales[pl.ds(where, 1), :], acc)
                 return acc
 
-            acc = lax.fori_loop(0, LANES // unroll, rows_body, jnp.zeros((1, LANES), jnp.float32))
+            acc = lax.fori_loop(0, BLOCK // unroll, rows_body, jnp.zeros((1, LANES), jnp.float32))
             scale_stage[field, base + n, group] = acc
 
-            if send:
-
-                @pl.when(step > first_group * count)
-                def _():
-                    before = step - 1
-                    send_block(field, base, count, before // count, before % count, source, which)
+            @pl.when((step > 0) & (step <= sent_groups * count))
+            def _():
+                before = step - 1
+                send_block(field, base, count, before // count, before % count, source, which)
 
             return carry
 
-        lax.fori_loop(first_group * count, last_group * count, step_body, 0)
-        if send:
-            send_block(field, base, count, last_group - 1, count - 1, source, which)
+        lax.fori_loop(0, groups * count, step_body, 0)
 
     own_plane(0).wait()
     plane_copy(0).wait_recv()
     row_transform_kernel(planes, (0,), ROW_OUTER // 2 + 1)
-    gather_blocks(0, 0, near, 0, groups, me, 0, True)
+    gather_blocks(0, 0, near, me, 0, groups)
+    send_block(0, 0, near, groups - 1, near - 1, me, 0)
     for place in range(1, 4):
         own_plane(place).wait()
         plane_copy(place).wait_recv()
     row_transform_kernel(planes, (1, 2, 3), ROW_OUTER)
-    gather_blocks(1, 0, peers, 0, groups - 1, me, 2, True)
-    gather_blocks(1, 0, peers, groups - 1, groups, me, 2, False)
+    gather_blocks(1, 0, peers, me, 2, early)
 
     for swap in range(2):
         far_copy(swap).wait_recv()
     row_transform_kernel(far_plane, (0,), ROW_OUTER // 2 + 1)
-    gather_blocks(0, near, near, 0, groups, far_me, 1, True)
-
-    def send_last(n, carry):
-        send_block(1, 0, peers, groups - 1, n, me, 2)
+    gather_blocks(0, near, near, far_me, 1, groups)
+    send_block(0, near, near, groups - 1, near - 1, far_me, 1)
+
+    def send_late(step, carry):
+        send_block(1, 0, peers, step // peers, step % peers, me, 2)
         return carry
 
-    lax.fori_loop(0, peers, send_last, 0)
+    lax.fori_loop(early * peers, groups * peers, send_late, 0)
 
     skip = inner // sub
     thinned = []
@@ -526,6 +527,29 @@
                 value = dot_nt(eye, ref[spin, :, first : first + LANES])
                 weights[span, spin * degrees : (spin + 1) * degrees] = jnp.where(keep, value, 0.0)
 
+    low_lanes = lane < BLOCK
+    per_plane = half // (LANES * degrees)
+
+    def wide_at(field, pair, j):
+        start = (pair % per_plane * degrees + j) * LANES
+        if not isinstance(start, int):
+            start = pl.multiple_of(start, LANES)
+        flat = pair // per_plane
+        return 2 * field + flat // 2, flat % 2, slice(None), pl.ds(start, LANES)
+
+    def widen(pair, carry):
+        first = weights[pl.ds(2 * pair, sub, peers), :]
+        second = weights[pl.ds(2 * pair + 1, sub, peers), :]
+        for field in range(2):
+            for j in range(degrees):
+                at = slice(field * degrees + j, field * degrees + j + 1)
+                planes[wide_at(field, pair, j)] = jnp.where(
+                    low_lanes, first[:, at], second[:, at]
+                ).astype(jnp.bfloat16)
+        return carry
+
+    lax.fori_loop(0, peers // split, widen, 0)
+
     raw_rows = raw.shape[1]
     raw_q = raw_rows // peers
     raw_steps = half // raw_rows
@@ -554,20 +578,31 @@
 
             raw_copy(ref, lanes, step).wait()
             base = pl.multiple_of(which * (sub // 2) + step * raw_q, raw_q)
-            for group in range(groups):
+            for wide in range(slots // LANES):
                 pieces = []
                 for top in range(0, raw_rows, raw_rows // 2):
                     source = raw[
-                        step % 2, top : top + raw_rows // 2, :, group * LANES : (group + 1) * LANES
+                        step % 2, top : top + raw_rows // 2, :, wide * LANES : (wide + 1) * LANES
                     ].reshape(raw_rows // 2 * degrees, LANES)
                     pieces.append(
                         jnp.dot(order[...], source, preferred_element_type=jnp.float32)
                     )
-                for k in range(peers):
+
+                def rows_of(k, j):
+                    start = (k * degrees + j) * small
+                    return jnp.concatenate(
+                        [piece[start : start + small] for piece in pieces], axis=0
+                    )
+
+                for pair in range(peers // split):
                     for j in range(degrees):
-                        start = (k * degrees + j) * small
-                        table[group, k, j, pl.ds(base, raw_q), :] = jnp.concatenate(
-                            [piece[start : start + small] for piece in pieces], axis=0
+                        first, second = rows_of(2 * pair, j), rows_of(2 * pair + 1, j)
+                        span = pl.ds(base, raw_q)
+                        table[2 * wide, pair, j, span, :] = jnp.where(
+                            low_lanes, first, pltpu.roll(second, BLOCK, 1)
+                        ).astype(jnp.bfloat16)
+                        table[2 * wide + 1, pair, j, span, :] = jnp.where(
+                            low_lanes, pltpu.roll(first, BLOCK, 1), second
                         ).astype(jnp.bfloat16)
             return carry
 
@@ -580,11 +615,10 @@
     scale_rows[...] = jnp.zeros_like(scale_rows)
 
     def column_block(position, carry):
-        early = position < groups - 1
-        scalar_turn = (position >= groups - 1) & (position < 2 * groups - 1)
+        scalar_turn = (position >= early) & (position < early + groups)
         field = jnp.where(scalar_turn, 0, 1)
         group = jnp.where(
-            early, position, jnp.where(scalar_turn, position - (groups - 1), groups - 1)
+            position < early, position, position - jnp.where(scalar_turn, early, groups)
         )
 
         @pl.when(field == 0)
@@ -621,7 +655,7 @@
         for a in range(peers):
             scale_rows[a : a + 1, :] = scale_recv[field, group, a]
         plain = scale_rows[...]
-        own_freq = owner_rows[pl.ds(me * groups + group, 1), :]
+        own_freq = owner_rows[pl.ds((me * groups + group) // split, 1), :]
         mirrored = ((own_freq & (ROW_OUTER - 1)) > ROW_OUTER // 2) & (field == 0)
         scale_cols[0] = plain.T
         scale_cols[1] = jnp.where(mirrored, -plain, plain).T
@@ -629,7 +663,9 @@
 
         def chunk(step, inner_carry):
             span = pl.ds(pl.multiple_of(step * step_rows, step_rows), step_rows)
-            sre, sim = scale_cols[0, span, :], scale_cols[1, span, :]
+            shift_by = group % split * BLOCK + step * step_rows
+            scale_span = pl.ds(pl.multiple_of(shift_by, step_rows), step_rows)
+            sre, sim = scale_cols[0, scale_span, :], scale_cols[1, scale_span, :]
             for first in range(0, sub, LANES):
                 items = []
                 for a in range(peers):
@@ -643,7 +679,7 @@
                         col_tc[k : k + 1, first : first + LANES],
                         col_ts[k : k + 1, first : first + LANES],
                     )
-                    start = pl.multiple_of(k % fold * LANES + step * step_rows, step_rows)
+                    start = pl.multiple_of(k % fold * BLOCK + step * step_rows, step_rows)
                     place = pl.ds(start, step_rows)
                     split_store(
                         x_high, x_low, (k // fold, place, slice(first, first + LANES)), real
@@ -654,38 +690,36 @@
                     )
             return inner_carry
 
-        lax.fori_loop(0, LANES // step_rows, chunk, 0)
+        lax.fori_loop(0, BLOCK // step_rows, chunk, 0)
         total[...] = jnp.zeros_like(total)
 
-        def block(k2, inner_carry):
-            where = (k2, slice(0, rows), slice(0, 2 * sub))
+        for k4 in range(peers // fold):
+            where = (k4, slice(0, rows), slice(0, 2 * sub))
             both = three_dots(col_mat_high, col_mat_low, x_high[where], x_low[where])
-            for r in range(fold):
-                k = k2 * fold + r
+            for r in range(fold // split):
+                pair = k4 * (fold // split) + r
                 span = slice(r * LANES, (r + 1) * LANES)
                 real, imag = both[:sub, span], both[sub:, span]
-                eight = weights[pl.ds(k, sub, peers), :]
-                four = jnp.where(field == 0, eight[:, :degrees], eight[:, degrees : 2 * degrees])
                 for j in range(degrees):
-                    weighted = table[group, k, j].astype(jnp.float32) * four[:, j : j + 1]
+                    wide = planes[wide_at(field, pair, j)].astype(jnp.float32)
+                    weighted = table[group, pair, j].astype(jnp.float32) * wide
                     for part, value in enumerate((real, imag)):
                         total[2 * j + part] += jnp.sum(
                             (weighted * value).reshape(sub // 8, 8, LANES), axis=0
                         )
-            return inner_carry
-
-        lax.fori_loop(0, peers // fold, block, 0)
-        sums[field, group] = jnp.sum(total[...], axis=1)
+        partial = jnp.sum(total[...], axis=1)
+        sums[field, group] = partial + pltpu.roll(partial, BLOCK, 1)
         return carry
 
     lax.fori_loop(0, 2 * groups, column_block, 0)
 
-    for group in range(groups):
-        slot_freq = signed(owner_rows[pl.ds(me * groups + group, 1), :], length)
+    for wide in range(slots // LANES):
+        slot_freq = signed(owner_rows[pl.ds(me * (slots // LANES) + wide, 1), :], length)
         turns = -slot_freq & 3
         phase_real = jnp.where(turns == 0, 1.0, jnp.where(turns == 2, -1.0, 0.0))
         phase_imag = jnp.where(turns == 1, 1.0, jnp.where(turns == 3, -1.0, 0.0))
-        scalar, spin = sums[0, group], sums[1, group]
+        scalar = jnp.where(low_lanes, sums[0, 2 * wide], sums[0, 2 * wide + 1])
+        spin = jnp.where(low_lanes, sums[1, 2 * wide], sums[1, 2 * wide + 1])
         for j in range(degrees):
             ell = jnp.full((1, LANES), ells[j], jnp.int32)
             ell_float = ell.astype(jnp.float32)
@@ -696,7 +730,7 @@
             re, im = 2 * j, 2 * j + 1
             inner_real = (-spin[im : im + 1] - coupling * scalar[re : re + 1]) * keep
             inner_imag = (spin[re : re + 1] - coupling * scalar[im : im + 1]) * keep
-            span = slice(group * LANES, (group + 1) * LANES)
+            span = slice(wide * LANES, (wide + 1) * LANES)
             out_ref[j, 0:1, span] = phase_real * inner_real - phase_imag * inner_imag
             out_ref[j, 1:2, span] = phase_real * inner_imag + phase_imag * inner_real
 
@@ -737,7 +771,7 @@
     length = 2 * half
     slots = deltas.shape[2] // 2
     degrees = deltas.shape[1]
-    groups = slots // LANES
+    groups = slots // BLOCK
     inner = length // ROW_OUTER
     sub = length // peers
     ids = np.arange(length)
@@ -771,11 +805,11 @@
             pltpu.VMEM((2 * sub, 2 * sub), bf),
             pltpu.VMEM((length, rows), jnp.int32),
             pltpu.VMEM((length, LANES), f32),
-            pltpu.VMEM((2, peers, groups, LANES, rows), jnp.int32),
+            pltpu.VMEM((2, peers, groups, BLOCK, rows), jnp.int32),
             pltpu.VMEM((2, peers, groups, 1, LANES), f32),
-            pltpu.VMEM((2, peers, groups, LANES, rows), jnp.int32),
+            pltpu.VMEM((2, peers, groups, BLOCK, rows), jnp.int32),
             pltpu.VMEM((2, groups, peers, 1, LANES), f32),
-            pltpu.VMEM((groups, peers, degrees, sub, LANES), bf),
+            pltpu.VMEM((groups, peers * BLOCK // LANES, degrees, sub, LANES), bf),
             pltpu.VMEM((2, raw_rows, degrees, slots), bf),
             pltpu.VMEM((width, width), bf),
             pltpu.VMEM(spins.shape, bf),

time: 212 us -> 210 us (level)
  no operation moved by 1% of the time
where the time goes in v3:
time: 210 us; the launch traced here: 209 us
  Pallas kernels  208 us (99%)
    pallas_call x1, Pallas kernels, pipeline_call(): pl.pallas_call(functools.partial(pipeline_kernel, peers), in_specs=[anywh...  208 us

profile of v3, /device:TPU:0, one launch (start us, length us, event | category | flops | bytes accessed | tf_op | source)
XLA Modules:
  0.0 209.1 jit_solution(15114716228267761951)
XLA Ops:
  0.0 207.8 %shard_map.118 = (f32[4,2,256]{2,1,0:T(2,128)}, bf16[2048,4,256]{2,1,0:T(4,128)(2,1)}) custom-call(bf16[4,512,2048]{2,1,0:T(8,128)(2,1)} %maps.1, bf16[2048,4,512]{2,1,0:T(4,128)(2,1)} %deltas.1, bf16[2,4,2048]{2,1,0:T(4,128)(2,1)} %bitcast.3, s32[4096]{0:T(1024)} %owner.1, s32[32,128]{1,0:T(8,128)} %bitcast.2, s32[4]{0:T(128)} %ells.1, f32[4]{0:T(128)} %priors.1, ...), custom_call_target="tpu_custom_call" | custom-call | tf_op jit(solution)/shard_map/pallas_call | solution.py:789
  207.8 1.3 copy.14

commit v4 on v3

--- a/solution.py
+++ b/solution.py
@@ -421,7 +421,7 @@
         )
 
     lane = lax.broadcasted_iota(jnp.int32, (1, LANES), 1)
-    unroll = 8
+    unroll = 16
     shift = ROW_OUTER.bit_length() - 1
 
     def send_block(field, base, count, group, n, source, which):

time: 210 us -> 210 us (level)
  no operation moved by 1% of the time
where the time goes in v4:
time: 210 us; the launch traced here: 209 us
  Pallas kernels  208 us (99%)
    pallas_call x1, Pallas kernels, pipeline_call(): pl.pallas_call(functools.partial(pipeline_kernel, peers), in_specs=[anywh...  208 us

profile of v4, /device:TPU:0, one launch (start us, length us, event | category | flops | bytes accessed | tf_op | source)
XLA Modules:
  0.0 209.4 jit_solution(15293907284060290352)
XLA Ops:
  0.0 208.1 %shard_map.118 = (f32[4,2,256]{2,1,0:T(2,128)}, bf16[2048,4,256]{2,1,0:T(4,128)(2,1)}) custom-call(bf16[4,512,2048]{2,1,0:T(8,128)(2,1)} %maps.1, bf16[2048,4,512]{2,1,0:T(4,128)(2,1)} %deltas.1, bf16[2,4,2048]{2,1,0:T(4,128)(2,1)} %bitcast.3, s32[4096]{0:T(1024)} %owner.1, s32[32,128]{1,0:T(8,128)} %bitcast.2, s32[4]{0:T(128)} %ells.1, f32[4]{0:T(128)} %priors.1, ...), custom_call_target="tpu_custom_call" | custom-call | tf_op jit(solution)/shard_map/pallas_call | solution.py:789
  208.1 1.3 copy.14
